TPU v7x, 32 devices: a whole 2x2x4 slice. The times are simulated.
32 devices in a mesh: batch: 2 (over x), col: 4 (over z), row: 4 (over y, core).
Axes of the slice: x: 2, y: 2, z: 4, core: 2. Of those that a mesh axis runs over, the one named last changes fastest.
Arguments:
- mat_blocks: float32 [49152, 64, 32], P(('batch', 'row'), 'col'), parts along dimension 0
Outputs:
- output 1: float32 [49152, 64, 32], P(('batch', 'row'), 'col'), parts along dimension 0
- output 2: float32 [256], P('batch'), parts along dimension 0
- output 3: float32 [8, 32, 32], P('batch'), parts along dimension 0
There are 2 independent parts. A program takes and returns all parts, laid end to end along the dimension named above; each array names one.
All inputs are finite; a program needn't handle non-finite values.
Results may differ from a plain program's by a relative error of at most 0.001.
Values sent between devices are 32-bit elements.
A program may use at most 1 GiB of HBM per device.

v0:
```python
import math
import jax
import jax.numpy as jnp
from jax import lax
from jax.sharding import PartitionSpec as P

PANELS = 4
HIGHEST = lax.Precision.HIGHEST


def mat_dot(left_mat, right_mat):
    return jnp.dot(left_mat, right_mat, precision=HIGHEST, preferred_element_type=jnp.float32)


def mat_einsum(einsum_form, left_mat, right_mat):
    return jnp.einsum(einsum_form, left_mat, right_mat, precision=HIGHEST, preferred_element_type=jnp.float32)


def apply_reflector(panel_work, tau_vec, column, col_idx, pivot_row, row_ids, tail_dots, pivot_line):
    col_ids = jnp.arange(panel_work.shape[1])
    alpha_val = lax.dynamic_index_in_dim(pivot_line, col_idx, keepdims=False)
    norm_val = jnp.sqrt(lax.dynamic_index_in_dim(tail_dots, col_idx, keepdims=False))
    beta_val = jnp.where(alpha_val >= 0.0, -norm_val, norm_val)
    tau_val = (beta_val - alpha_val) / beta_val
    scale_val = 1.0 / (alpha_val - beta_val)
    refl_vec = jnp.where(row_ids > pivot_row, column * scale_val, jnp.where(row_ids == pivot_row, 1.0, 0.0))
    refl_dot = scale_val * (tail_dots - alpha_val * pivot_line) + pivot_line
    refl_dot = jnp.where(col_ids > col_idx, refl_dot, 0.0)
    new_col = jnp.where(row_ids < pivot_row, column, jnp.where(row_ids == pivot_row, beta_val, refl_vec))
    panel_work = jnp.where(col_ids[None, :] == col_idx, new_col[:, None], panel_work - tau_val * refl_vec[:, None] * refl_dot[None, :])
    tau_vec = jnp.where(col_ids == col_idx, tau_val, tau_vec)
    return panel_work, tau_vec


def factor_panel_rows(panel_in, row_base, pivot_base):
    local_rows, block_width = panel_in.shape
    row_ids = row_base + jnp.arange(local_rows)

    def column_step(col_idx, loop_state):
        panel_work, tau_vec = loop_state
        pivot_row = pivot_base + col_idx
        column = lax.dynamic_index_in_dim(panel_work, col_idx, axis=1, keepdims=False)
        tail_col = jnp.where(row_ids >= pivot_row, column, 0.0)
        local_pivot = jnp.clip(pivot_row - row_base, 0, local_rows - 1)
        holds_pivot = (pivot_row >= row_base) & (pivot_row < row_base + local_rows)
        pivot_line = lax.dynamic_index_in_dim(panel_work, local_pivot, axis=0, keepdims=False)
        pivot_line = jnp.where(holds_pivot, pivot_line, 0.0)
        packed = jnp.concatenate([mat_dot(tail_col[None, :], panel_work)[0], pivot_line])
        packed = lax.psum(packed, 'row')
        return apply_reflector(panel_work, tau_vec, column, col_idx, pivot_row, row_ids, packed[:block_width], packed[block_width:])

    return lax.fori_loop(0, block_width, column_step, (panel_in, jnp.zeros((block_width,), jnp.float32)))


def tfactor_from_gram(gram_mat, tau_vec):
    block_width = gram_mat.shape[0]
    col_ids = jnp.arange(block_width)
    step_mat = -tau_vec[:, None] * jnp.where(col_ids[None, :] > col_ids[:, None], gram_mat, 0.0)
    eye_mat = jnp.eye(block_width, dtype=jnp.float32)
    inv_acc = eye_mat + step_mat
    power_mat = step_mat
    for level_num in range(max(1, math.ceil(math.log2(block_width))) - 1):
        power_mat = mat_dot(power_mat, power_mat)
        inv_acc = mat_dot(inv_acc, eye_mat + power_mat)
    return inv_acc * tau_vec[None, :]


def solution(mesh):
    col_count = mesh.shape['col']
    block_spec = P(('batch', 'row'), 'col', None)

    def device_fn(a_local):
        local_rows, local_blocks, block_width = a_local.shape
        col_rank = lax.axis_index('col')
        row_base = lax.axis_index('row') * local_rows
        row_ids = row_base + jnp.arange(local_rows)
        col_ids = jnp.arange(block_width)
        global_ids = jnp.arange(local_blocks) * col_count + col_rank
        tau_list = []
        tfac_list = []
        for panel_idx in range(PANELS):
            owner_col = panel_idx % col_count
            block_pos = panel_idx // col_count
            pivot_ids = panel_idx * block_width + col_ids
            panel_out, tau_vec = factor_panel_rows(a_local[:, block_pos, :], row_base, panel_idx * block_width)
            refl_mat = jnp.where(row_ids[:, None] > pivot_ids[None, :], panel_out, jnp.where(row_ids[:, None] == pivot_ids[None, :], 1.0, 0.0))
            gram_mat = lax.psum(mat_einsum('rk,rj->kj', refl_mat, refl_mat), 'row')
            t_factor = tfactor_from_gram(gram_mat, tau_vec)
            packed = jnp.concatenate([refl_mat, t_factor], axis=0)
            packed = lax.psum(jnp.where(col_rank == owner_col, packed, 0.0), 'col')
            refl_mat = packed[:local_rows]
            t_factor = packed[local_rows:]
            w_summed = lax.psum(mat_einsum('rk,rbc->kbc', refl_mat, a_local), 'row')
            w_mat = mat_einsum('kj,kbc->jbc', t_factor, w_summed)
            w_mat = jnp.where((global_ids > panel_idx)[None, :, None], w_mat, 0.0)
            a_local = a_local - mat_einsum('rj,jbc->rbc', refl_mat, w_mat)
            a_local = jnp.where((global_ids == panel_idx)[None, :, None], panel_out[:, None, :], a_local)
            tau_list.append(jnp.diagonal(t_factor))
            tfac_list.append(t_factor)
        return a_local, jnp.concatenate(tau_list), jnp.stack(tfac_list)

    return jax.shard_map(device_fn, mesh=mesh, in_specs=(block_spec,), out_specs=(block_spec, P('batch'), P('batch', None, None)), check_vma=False)
```

profile of v0, /device:TPU:1, one launch (start us, length us, event | category | flops | bytes accessed | tf_op | source)
XLA Modules:
  0.0 2159.5 jit_solution(8916022763796882147)
XLA Ops:
  8.4 391.6 %while.76 = (s32[]{:T(128)}, f32[6144,32]{0,1:T(8,128)S(1)}, f32[32]{0:T(128)S(1)}, s32[]{:T(128)}, s32[]{:T(128)}, /*index=5*/s32[]{:T(128)}, s32[]{:T(128)}, s32[]{:T(128)}, f32[]{:T(128)}, f32[]{:T(128)}) while((s32[]{:T(128)}, f32[6144,32]{0,1:T(8,128)S(1)}, f32[32]{0:T(128)S(1)}, s32[]{:T(128)}, ...), condition=%wide.region_2.3_spmd.clone.clone.clone, body=%wide.region_0.2_spmd.clone.clone.clone.sunk | while | flops 3035632 | bytes 2645027 | solution.py:52
  9.6 6.4 psum.160
  22.2 7.0 psum.160
  71.3 6.4 psum.160
  95.9 6.2 psum.160
  144.3 6.5 psum.160
  217.6 6.2 psum.160
  400.9 9.5 psum.132
  412.9 46.5 %all-reduce.9.cloned.1.call-done = f32[6176,32]{0,1:T(8,128)} async-done(((f32[6176,32]{0,1:T(8,128)}), f32[6176,32]{0,1:T(8,128)}) %all-reduce.9.cloned.1.call-update) | async-done | bytes 790544 | tf_op jit(solution)/shard_map/psum | solution.py:90
  459.3 31.7 %fusion.38 = f32[32,16,32]{2,0,1:T(8,128)} fusion(f32[6144,16,32]{0,2,1:T(8,128)} %param.9, f32[6176,32]{0,1:T(8,128)} %all-reduce.9.cloned.1.call-done), kind=kOutput, calls=%fused_computation.117 | convolution fusion | flops 1207959552 | bytes 13434880 | tf_op jit(solution)/shard_map/rk,rbc->kbc/dot_general | solution.py:16
  491.6 29.9 %all-reduce.11.cloned.1.call-done = f32[32,16,32]{2,0,1:T(8,128)} async-done(((f32[32,16,32]{2,0,1:T(8,128)}), f32[32,16,32]{2,0,1:T(8,128)}) %all-reduce.11.cloned.1.call-update) | async-done | bytes 65552 | tf_op jit(solution)/shard_map/psum | solution.py:93
  522.9 10.1 fusion.49
  533.0 6.7 subtract_select_fusion.7
  544.5 396.2 %while.77 = (s32[]{:T(128)}, f32[6144,32]{0,1:T(8,128)S(1)}, f32[32]{0:T(128)S(1)}, s32[]{:T(128)}, s32[]{:T(128)}, /*index=5*/s32[]{:T(128)}, s32[]{:T(128)}, s...) while((s32[]{:T(128)}, f32[6144,32]{0,1:T(8,128)S(1)}, f32[32]{0:T(128)S(1)}, ...), condition=%wide.region_8.9_spmd.clone.clone.clone, body=%wide.region_6.8_spmd.clone.clone.clone.sunk | while | flops 3035633 | bytes 2645047 | solution.py:52
  545.6 7.2 psum.161
  595.5 6.4 psum.161
  620.5 6.2 psum.161
  669.6 6.5 psum.161
  743.8 6.2 psum.161
  941.7 9.7 psum.135
  953.9 46.3 %all-reduce.13.cloned.1.call-done = f32[6176,32]{0,1:T(8,128)} async-done(((f32[6176,32]{0,1:T(8,128)}), f32[6176,32]{0,1:T(8,128)}) %all-reduce.13.cloned.1.call-update) | async-done | bytes 790544 | tf_op jit(solution)/shard_map/psum | solution.py:90
  1000.2 31.7 %fusion.36 = f32[32,16,32]{2,0,1:T(8,128)} fusion(f32[6144,16,32]{0,2,1:T(8,128)} %copy-done.2, f32[6176,32]{0,1:T(8,128)} %all-reduce.13.cloned.1.call-done), kind=kOutput, calls=%fused_computation.115 | convolution fusion | flops 1207959552 | bytes 13434880 | tf_op jit(solution)/shard_map/rk,rbc->kbc/dot_general | solution.py:16
  1032.2 30.1 %all-reduce.15.cloned.1.call-done = f32[32,16,32]{2,0,1:T(8,128)} async-done(((f32[32,16,32]{2,0,1:T(8,128)}), f32[32,16,32]{2,0,1:T(8,128)}) %all-reduce.15.cloned.1.call-update) | async-done | bytes 65552 | tf_op jit(solution)/shard_map/psum | solution.py:93
  1063.8 10.1 fusion.46
  1073.8 7.0 subtract_select_fusion.6
  1085.6 396.2 %while.78 = (s32[]{:T(128)}, f32[6144,32]{0,1:T(8,128)S(1)}, f32[32]{0:T(128)S(1)}, s32[]{:T(128)}, s32[]{:T(128)}, /*index=5*/s32[]{:T(128)}, s32[]{:T(128)}, s...) while((s32[]{:T(128)}, f32[6144,32]{0,1:T(8,128)S(1)}, ...), condition=%wide.region_14.15_spmd.clone.clone.clone, body=%wide.region_12.14_spmd.clone.clone.clone.sunk | while | flops 3035633 | bytes 2645047 | solution.py:52
  1086.7 7.2 psum.162
  1136.6 6.4 psum.162
  1161.6 6.2 psum.162
  1210.7 6.5 psum.162
  1284.9 6.2 psum.162
  1482.8 9.7 psum.138
  1495.0 46.2 %all-reduce.17.cloned.1.call-done = f32[6176,32]{0,1:T(8,128)} async-done(((f32[6176,32]{0,1:T(8,128)}), f32[6176,32]{0,1:T(8,128)}) %all-reduce.17.cloned.1.call-update) | async-done | bytes 790544 | tf_op jit(solution)/shard_map/psum | solution.py:90
  1541.3 31.6 %fusion.34 = f32[32,16,32]{2,0,1:T(8,128)} fusion(f32[6144,16,32]{0,2,1:T(8,128)} %copy-done.1, f32[6176,32]{0,1:T(8,128)} %all-reduce.17.cloned.1.call-done), kind=kOutput, calls=%fused_computation.113 | convolution fusion | flops 1207959552 | bytes 13434880 | tf_op jit(solution)/shard_map/rk,rbc->kbc/dot_general | solution.py:16
  1573.2 30.2 %all-reduce.19.cloned.1.call-done = f32[32,16,32]{2,0,1:T(8,128)} async-done(((f32[32,16,32]{2,0,1:T(8,128)}), f32[32,16,32]{2,0,1:T(8,128)}) %all-reduce.19.cloned.1.call-update) | async-done | bytes 65552 | tf_op jit(solution)/shard_map/psum | solution.py:93
  1604.8 11.2 fusion.43
  1616.0 6.8 subtract_select_fusion.5
  1627.7 378.1 %while.79 = (s32[]{:T(128)}, f32[6144,32]{0,1:T(8,128)S(1)}, f32[32]{0:T(128)S(1)}, s32[]{:T(128)}, s32[]{:T(128)}, /*index=5*/s32[]{:T(128)}, s32[]{:T(128)}, s...) while((s32[]{:T(128)}, f32[6144,32]{0,1:T(8,128)S(1)}, ...), condition=%wide.region_20.21_spmd.clone.clone.clone, body=%wide.region_18.20_spmd.clone.clone.clone.sunk | while | flops 3035633 | bytes 2645047 | solution.py:52
  1628.8 7.2 psum.163
  1676.4 6.4 psum.163
  1700.2 6.2 psum.163
  1747.0 6.5 psum.163
  2006.7 9.7 psum.141
  2021.7 43.7 %all-reduce.21.cloned.1.call-done = f32[6176,32]{0,1:T(8,128)} async-done(((f32[6176,32]{0,1:T(8,128)}), f32[6176,32]{0,1:T(8,128)}) %all-reduce.21.cloned.1.call-update) | async-done | bytes 790544 | tf_op jit(solution)/shard_map/psum | solution.py:90
  2067.0 31.9 %fusion.32 = f32[32,16,32]{2,0,1:T(8,128)} fusion(f32[6144,16,32]{0,2,1:T(8,128)} %copy-done, f32[6176,32]{0,1:T(8,128)} %all-reduce.21.cloned.1.call-done), kind=kOutput, calls=%fused_computation.111 | convolution fusion | flops 1207959552 | bytes 13434880 | tf_op jit(solution)/shard_map/rk,rbc->kbc/dot_general | solution.py:16
  2100.2 29.1 %all-reduce.23.cloned.1.call-done = f32[32,16,32]{2,0,1:T(8,128)} async-done(((f32[32,16,32]{2,0,1:T(8,128)}), f32[32,16,32]{2,0,1:T(8,128)}) %all-reduce.23.cloned.1.call-update) | async-done | bytes 65552 | tf_op jit(solution)/shard_map/psum | solution.py:93
  2130.7 10.1 fusion.40
  2140.8 11.4 subtract_select_fusion.4
  (2016 shorter events, 1121.7 us)
Async XLA Ops:
  7.2 452.2 %all-reduce.9.cloned.1.call-start = ((), (), s32[]{:S(2)}) async-start(), calls=%async_computation | async-start | bytes 1605632 | tf_op jit(solution)/shard_map/psum | solution.py:90
  412.8 108.7 %all-reduce.11.cloned.1.call-start = ((), (), s32[]{:S(2)}) async-start(), calls=%async_computation.1 | async-start | bytes 524288 | tf_op jit(solution)/shard_map/psum | solution.py:93
  459.3 62.1 %copy-start.3 = (f32[6176,32]{0,1:T(8,128)S(1)}, f32[6176,32]{0,1:T(8,128)}, u32[]{:S(2)}) copy-start(f32[6176,32]{0,1:T(8,128)} %all-reduce.9.cloned.1.call-done) | copy-start | bytes 2371588
  491.0 509.1 %all-reduce.13.cloned.1.call-start = ((), (), s32[]{:S(2)}) async-start(), calls=%async_computation.2 | async-start | bytes 1605632 | tf_op jit(solution)/shard_map/psum | solution.py:90
  539.7 4.8 copy-start.2
  953.8 108.5 %all-reduce.15.cloned.1.call-start = ((), (), s32[]{:S(2)}) async-start(), calls=%async_computation.3 | async-start | bytes 524288 | tf_op jit(solution)/shard_map/psum | solution.py:93
  1000.2 62.1 %copy-start.4 = (f32[6176,32]{0,1:T(8,128)S(1)}, f32[6176,32]{0,1:T(8,128)}, u32[]{:S(2)}) copy-start(f32[6176,32]{0,1:T(8,128)} %all-reduce.13.cloned.1.call-done) | copy-start | bytes 2371588
  1031.9 509.3 %all-reduce.17.cloned.1.call-start = ((), (), s32[]{:S(2)}) async-start(), calls=%async_computation.4 | async-start | bytes 1605632 | tf_op jit(solution)/shard_map/psum | solution.py:90
  1080.8 4.8 copy-start.1
  1494.9 108.4 %all-reduce.19.cloned.1.call-start = ((), (), s32[]{:S(2)}) async-start(), calls=%async_computation.5 | async-start | bytes 524288 | tf_op jit(solution)/shard_map/psum | solution.py:93
  1572.9 492.5 %all-reduce.21.cloned.1.call-start = ((), (), s32[]{:S(2)}) async-start(), calls=%async_computation.6 | async-start | bytes 1605632 | tf_op jit(solution)/shard_map/psum | solution.py:90
  1622.8 4.8 copy-start
  2018.8 110.5 %all-reduce.23.cloned.1.call-start = ((), (), s32[]{:S(2)}) async-start(), calls=%async_computation.7 | async-start | bytes 524288 | tf_op jit(solution)/shard_map/psum | solution.py:93
  2065.5 63.8 %copy-start.5 = (f32[6176,32]{0,1:T(8,128)S(1)}, f32[6176,32]{0,1:T(8,128)}, u32[]{:S(2)}) copy-start(f32[6176,32]{0,1:T(8,128)} %all-reduce.21.cloned.1.call-done) | copy-start | bytes 2371588
Sparse Core Ops, SparseCore 0:
  412.9 46.3 all-reduce.8
  491.2 30.2 all-reduce.10
  954.0 46.1 all-reduce.12
  1032.0 30.2 all-reduce.14
  1495.0 46.1 all-reduce.16
  1573.1 30.2 all-reduce.18
  2018.9 46.5 all-reduce.20
  2099.0 30.2 all-reduce.22
where the time goes:
time: 2180 us; the launch traced here: 2160 us
  blocking collectives  805 us (37%)
  loops' own time  352 us (16%)
  waiting for transfers between devices  302 us (14%)
  matrix products  273 us (13%)
  other arithmetic  222 us (10%)
  local copies, waits for them, and re-layouts  189 us (9%)
    psum x128, blocking collectives, column_step(): packed = lax.psum(packed, 'row')  767 us
    another operation x4, loops' own time, factor_panel_rows(): lax.fori_loop(0, block_width, column_step, (panel_in, jnp.zeros((block_wi...  352 us
    psum x4, waiting for transfers between devices, device_fn(): packed = lax.psum(jnp.where(col_rank == owner_col, packed, 0.0), 'col')  183 us
    dot_general x12, matrix products, mat_einsum(): jnp.einsum(einsum_form, left_mat, right_mat, precision=HIGHEST, preferred...  135 us
    psum x4, waiting for transfers between devices, device_fn(): w_summed = lax.psum(mat_einsum('rk,rbc->kbc', refl_mat, a_local), 'row')  119 us
    dot_general x160, matrix products, mat_dot(): jnp.dot(left_mat, right_mat, precision=HIGHEST, preferred_element_type=jn...  96.7 us
    select_n x128, other arithmetic, apply_reflector(): refl_dot = jnp.where(col_ids > col_idx, refl_dot, 0.0)  92.2 us
    dynamic_slice x128, local copies, waits for them, and re-layouts, apply_reflector(): alpha_val = lax.dynamic_index_in_dim(pivot_line, col_idx, keepdims=False)  79.6 us
  transfers between devices with their start and end apart: 8, of which 8 were waited for; matrix products, arithmetic and copies ran while one was open for 0% of the time, Pallas kernels for 0%

commit v1 on v0

v1 whole, which is shorter than its diff:
```python
import functools
import jax
import jax.numpy as jnp
from jax import lax
from jax.experimental import pallas as pl
from jax.experimental.pallas import tpu as pltpu
from jax.sharding import PartitionSpec as P

PANELS = 4
WIDTH = 32
NPAN = PANELS * WIDTH
HIGHEST = lax.Precision.HIGHEST
NN = (((1,), (0,)), ((), ()))
NT = (((1,), (1,)), ((), ()))
TN = (((0,), (0,)), ((), ()))


def dot(left, right, dims=NN):
    return lax.dot_general(left, right, dims, precision=HIGHEST, preferred_element_type=jnp.float32)


def lane_col(mat, pos):
    return jnp.broadcast_to(mat[:, pos:pos + 1], mat.shape)


def factor_loop(gram, work, rmat):
    lanes = lax.broadcasted_iota(jnp.int32, (1, NPAN), 1)
    for panel in range(PANELS):
        base = panel * WIDTH
        rows = NPAN - base
        subs = lax.broadcasted_iota(jnp.int32, (rows, NPAN), 0) + base
        lane2 = lax.broadcasted_iota(jnp.int32, (rows, NPAN), 1)

        def step(k, carry):
            g = gram[base:, :]
            w = work[base:, :]
            hit = lane2 == k
            gcol = jnp.sum(jnp.where(hit, g, 0.0), axis=1, keepdims=True)
            acol = jnp.sum(jnp.where(hit, w, 0.0), axis=1, keepdims=True)
            grow = gram[pl.ds(k, 1), :]
            wrow = work[pl.ds(k, 1), :]
            here = lanes == k
            gkk = jnp.sum(jnp.where(here, grow, 0.0), axis=1, keepdims=True)
            alpha = jnp.sum(jnp.where(here, wrow, 0.0), axis=1, keepdims=True)
            norm = jnp.sqrt(jnp.maximum(gkk, alpha * alpha))
            beta = jnp.where(alpha >= 0.0, -norm, norm)
            scale = 1.0 / (alpha - beta)
            rb = 1.0 / beta
            rrow = grow * rb
            rcol = gcol * rb
            dcol = jnp.where(subs[:, :1] > k, acol - rcol, 0.0)
            prow = jnp.where(here, scale, scale * wrow)
            gram[base:, :] = g - rcol * rrow
            work[base:, :] = jnp.where(hit & (subs > k), 0.0, w) - dcol * prow
            work[pl.ds(k, 1), :] = prow
            rmat[pl.ds(k, 1), :] = jnp.where(here, beta, jnp.where(lanes > k, rrow, 0.0))
            return carry

        lax.fori_loop(base, base + WIDTH, step, 0)


def upper_inverse(mat):
    rows = lax.broadcasted_iota(jnp.int32, mat.shape, 0)
    cols = lax.broadcasted_iota(jnp.int32, mat.shape, 1)
    inv = jnp.where(rows == cols, 1.0 / jnp.where(rows == cols, mat, 1.0), 0.0)
    size = 1
    while size < mat.shape[0]:
        pair = (rows // (2 * size) == cols // (2 * size)) & ((rows // size) % 2 == 0) & ((cols // size) % 2 == 1)
        off = jnp.where(pair, mat, 0.0)
        inv = inv - dot(dot(inv, off), inv)
        size *= 2
    return inv


def factor_kernel(pay_ref, xt_ref, top_ref, t_ref, tau_ref, gram, work, rmat):
    nloc = xt_ref.shape[0]
    col = lax.axis_index('col')
    gram[...] = pay_ref[nloc:nloc + NPAN, :]
    work[...] = pay_ref[2 * nloc + NPAN:, :]
    factor_loop(gram, work, rmat)
    rows = lax.broadcasted_iota(jnp.int32, (NPAN, NPAN), 0)
    cols = lax.broadcasted_iota(jnp.int32, (NPAN, NPAN), 1)
    done = work[...]
    rfac = rmat[...]
    cst = jnp.where(cols <= rows, done, 0.0)
    v1t = jnp.where(cols > rows, done, jnp.where(cols == rows, 1.0, 0.0))
    tinv = -dot(dot(v1t, rfac), cst, NT)
    tinv = jnp.where(cols >= rows, tinv, 0.0)
    tmat = upper_inverse(tinv)
    for panel in range(PANELS):
        base = panel * WIDTH
        t_ref[panel] = tmat[base:base + WIDTH, base:base + WIDTH]
    tau_ref[...] = jnp.sum(jnp.where(cols == rows, tmat, 0.0), axis=0, keepdims=True)
    h_t = pay_ref[:nloc, :]
    top_t = pay_ref[nloc + NPAN:2 * nloc + NPAN, :]
    pan_t = pay_ref[2 * nloc + NPAN:, :]
    m1 = dot(v1t, tmat, TN)
    m2 = dot(cst, tmat, TN)
    k1 = m1 - dot(pan_t, m2, TN)
    yt = dot(top_t, k1) + dot(h_t, m2)
    xt_ref[...] = dot(yt, cst)
    top_ref[...] = top_t - dot(yt, v1t)
    final = jnp.where(cols > rows, done, 0.0) + rfac.T
    work[...] = final
    gram[...] = -cst
    base = pl.multiple_of(col * WIDTH, WIDTH)
    xt_ref[:WIDTH, :] = gram[pl.ds(base, WIDTH), :]
    top_ref[:WIDTH, :] = work[pl.ds(base, WIDTH), :]


def update_kernel(b_ref, p_ref, xt_ref, top_ref, out_ref):
    prod = dot(xt_ref[...], p_ref[...])
    out_ref[:WIDTH, :] = -prod[:WIDTH, :]
    out_ref[WIDTH:, :] = b_ref[WIDTH:, :] - prod[WIDTH:, :]

    @pl.when((lax.axis_index('row') == 0) & (pl.program_id(0) == 0))
    def _():
        out_ref[:, :NPAN] = top_ref[...]


def solution(mesh):
    block_spec = P(('batch', 'row'), 'col', None)

    def device_fn(a_local):
        nrow, nblk, width = a_local.shape
        nloc = nblk * width
        b_t = a_local.transpose(1, 2, 0).reshape(nloc, nrow)
        row = lax.axis_index('row')
        p_t = lax.all_gather(b_t[:width], 'col', axis=0, tiled=True)
        h_t = dot(b_t, p_t, NT)
        g_t = dot(p_t, p_t, NT)
        tops = jnp.concatenate([b_t[:, :NPAN], p_t[:, :NPAN]], axis=0)
        tops = jnp.where(row == 0, tops, 0.0)
        pay = lax.psum(jnp.concatenate([h_t, g_t, tops], axis=0), 'row')
        full = lambda shape: jax.ShapeDtypeStruct(shape, jnp.float32)
        xt, top, tfac, tau = pl.pallas_call(
            factor_kernel,
            out_shape=(full((nloc, NPAN)), full((nloc, NPAN)), full((PANELS, WIDTH, WIDTH)), full((1, NPAN))),
            scratch_shapes=[pltpu.VMEM((NPAN, NPAN), jnp.float32)] * 3,
            name='factor',
        )(pay)
        chunk = 512
        out = pl.pallas_call(
            update_kernel,
            grid=(nrow // chunk,),
            in_specs=[
                pl.BlockSpec((nloc, chunk), lambda i: (0, i)),
                pl.BlockSpec((NPAN, chunk), lambda i: (0, i)),
                pl.BlockSpec((nloc, NPAN), lambda i: (0, 0)),
                pl.BlockSpec((nloc, NPAN), lambda i: (0, 0)),
            ],
            out_specs=pl.BlockSpec((nloc, chunk), lambda i: (0, i)),
            out_shape=full((nloc, nrow)),
            name='update',
        )(b_t, p_t, xt, top)
        return out.reshape(nblk, width, nrow).transpose(2, 0, 1), tau.reshape(NPAN), tfac

    return jax.shard_map(device_fn, mesh=mesh, in_specs=(block_spec,), out_specs=(block_spec, P('batch'), P('batch', None, None)), check_vma=False)
```

time: 2180 us -> 176 us (0.08)
  blocking collectives: 805 us -> 0 us
  loops' own time: 352 us -> 0 us
  matrix products: 273 us -> 18 us
  other arithmetic: 222 us -> 0.9 us
  waiting for transfers between devices: 302 us -> 96.1 us
  local copies, waits for them, and re-layouts: 189 us -> 4.03 us
  Pallas kernels: 0 us -> 39.9 us
    psum x132 -> x0, blocking collectives: 805 us -> none  [the longest x128 767 us: column_step(): packed = lax.psum(packed, 'row')]
    another operation x4 -> x0, loops' own time: 352 us -> none  [factor_panel_rows(): lax.fori_loop(0, block_width, column_step, (panel_in, jnp.zeros((block_wi...]
    psum x8 -> x1, waiting for transfers between devices: 302 us -> 31.6 us  [device_fn(): pay = lax.psum(jnp.concatenate([h_t, g_t, tops], axis=0), 'row')]
    dot_general x172 -> x2, matrix products: 232 us -> 18 us  [dot(): lax.dot_general(left, right, dims, precision=HIGHEST, preferred_element_t...]
    select_n x652 -> x1, other arithmetic: 207 us -> 0.02 us  [device_fn(): tops = jnp.where(row == 0, tops, 0.0)]
    dynamic_slice x384 -> x0, local copies, waits for them, and re-layouts: 158 us -> none  [the longest x128 79.6 us: apply_reflector(): alpha_val = lax.dynamic_index_in_dim(pivot_line, col_idx, keepdims=False)]
    all_gather x0 -> x1, waiting for transfers between devices: none -> 64.4 us  [device_fn(): p_t = lax.all_gather(b_t[:width], 'col', axis=0, tiled=True)]
    unnamed x4 -> x0, matrix products: 41.4 us -> none
  transfers between devices with their start and end apart: 8 -> 2, of which waited for: 8 -> 2; matrix products, arithmetic and copies ran while one was open for 0% -> 1% of each run, Pallas kernels for 0% -> 0%
where the time goes in v1:
time: 176 us; the launch traced here: 173 us
  waiting for transfers between devices  96.1 us (55%)
  Pallas kernels  39.9 us (23%)
  matrix products  18 us (10%)
  between operations  14.1 us (8%)
  local copies, waits for them, and re-layouts  4.03 us (2%)
    all_gather x1, waiting for transfers between devices, device_fn(): p_t = lax.all_gather(b_t[:width], 'col', axis=0, tiled=True)  64.4 us
    psum x1, waiting for transfers between devices, device_fn(): pay = lax.psum(jnp.concatenate([h_t, g_t, tops], axis=0), 'row')  31.6 us
    pallas_call x1, Pallas kernels, device_fn(): pl.pallas_call(factor_kernel, out_shape=(full((nloc, NPAN)), full((nloc,...  21.8 us
    pallas_call x1, Pallas kernels, device_fn(): pl.pallas_call(update_kernel, grid=(nrow // chunk,), in_specs=[pl.BlockSp...  18.1 us
    dot_general x2, matrix products, dot(): lax.dot_general(left, right, dims, precision=HIGHEST, preferred_element_t...  18 us
  transfers between devices with their start and end apart: 2, of which 2 were waited for; matrix products, arithmetic and copies ran while one was open for 1% of the time, Pallas kernels for 0%

profile of v1, /device:TPU:1, one launch (start us, length us, event | category | flops | bytes accessed | tf_op | source)
XLA Modules:
  0.0 173.1 jit_solution(12778825518585458653)
XLA Ops:
  7.2 0.0 all-gather.3.cloned.1.call-start
  7.2 2.1 %slice.16 = f32[1,32,6144]{2,1,0:T(8,128)} slice(f32[16,32,6144]{2,1,0:T(8,128)} %bitcast.13), slice={[0:1], [0:32], [0:6144]} | slice | bytes 1572864 | tf_op jit(solution)/shard_map/slice | solution.py:129
  9.3 0.0 all-gather.3.cloned.1.call-update
  9.3 0.0 all-reduce.2.cloned.1.call-start
  9.4 1.0 slice.17
  10.3 64.4 %all-gather.3.cloned.1.call-done = f32[1,128,6144]{2,1,0:T(8,128)} async-done(((f32[1,32,6144]{2,1,0:T(8,128)}), f32[1,128,6144]{2,1,0:T(8,128)}) %all-gather.3.cloned.1.call-update) | async-done | bytes 3145744 | tf_op jit(solution)/shard_map/all_gather | solution.py:129
  74.8 0.0 copy-start
  74.8 1.0 slice.18
  75.8 5.5 %fusion = f32[128,128]{1,0:T(8,128)S(1)} fusion(f32[1,128,6144]{2,1,0:T(8,128)} %all-gather.3.cloned.1.call-done), kind=kOutput, calls=%fused_computation.2 | convolution fusion | flops 1207959552 | bytes 3211264 | tf_op jit(solution)/shard_map/dot_general | solution.py:19
  81.3 0.0 copy-done
  81.3 12.5 %fusion.2 = f32[512,128]{1,0:T(8,128)S(1)} fusion(f32[512,6144]{1,0:T(8,128)} %bitcast.15, f32[1,128,6144]{2,1,0:T(8,128)S(1)} %copy-done), kind=kOutput, calls=%fused_computation.4 | convolution fusion | flops 4831838208 | bytes 15990784 | tf_op jit(solution)/shard_map/dot_general | solution.py:19
  93.8 0.9 pad_maximum_fusion
  94.7 0.0 all-reduce.2.cloned.1.call-update
  94.7 31.6 %all-reduce.2.cloned.1.call-done.pay_ref = f32[1280,128]{1,0:T(8,128)} async-done(((f32[1280,128]{1,0:T(8,128)}), f32[1280,128]{1,0:T(8,128)}) %all-reduce.2.cloned.1.call-update) | async-done | bytes 655376 | tf_op jit(solution)/shard_map/psum | solution.py:134
  126.3 21.8 %factor.1 = (f32[512,128]{1,0:T(8,128)}, f32[512,128]{1,0:T(8,128)}, f32[4,32,32]{2,1,0:T(8,128)}, f32[1,128]{1,0:T(1,128)}) custom-call(f32[1280,128]{1,0:T(8,128)} %all-reduce.2.cloned.1.call-done.pay_ref), custom_call_target="tpu_custom_call" | custom-call | tf_op jit(solution)/shard_map/factor/pallas_call | solution.py:136
  148.1 18.1 %update.1 = f32[512,6144]{1,0:T(8,128)} custom-call(f32[512,6144]{1,0:T(8,128)} %bitcast.16, f32[128,6144]{1,0:T(8,128)} %bitcast.18, f32[512,128]{1,0:T(8,128)} %get-tuple-element.7.xt_ref, f32[512,128]{1,0:T(8,128)} %get-tuple-element.8.top_ref), custom_call_target="tpu_custom_call" | custom-call | tf_op jit(solution)/shard_map/update/pallas_call | solution.py:143
  (1 shorter events, 0.0 us)
Async XLA Ops:
  7.2 67.6 %all-gather.3.cloned.1.call-start = ((), (), s32[]{:S(2)}) async-start(), calls=%async_computation.1 | async-start | bytes 3932160 | tf_op jit(solution)/shard_map/all_gather | solution.py:129
  9.3 117.0 %all-reduce.2.cloned.1.call-start = ((), (), s32[]{:S(2)}) async-start(), calls=%async_computation | async-start | bytes 1310720 | tf_op jit(solution)/shard_map/psum | solution.py:134
  74.8 6.5 %copy-start = (f32[1,128,6144]{2,1,0:T(8,128)S(1)}, f32[1,128,6144]{2,1,0:T(8,128)}, u32[]{:S(2)}) copy-start(f32[1,128,6144]{2,1,0:T(8,128)} %all-gather.3.cloned.1.call-done) | copy-start | bytes 9437188
Sparse Core Ops, SparseCore 0:
  10.1 64.6 all-gather.2
  94.8 31.4 all-reduce.1

commit v2 on v1

--- a/solution.py
+++ b/solution.py
@@ -19,11 +19,15 @@
     return lax.dot_general(left, right, dims, precision=HIGHEST, preferred_element_type=jnp.float32)
 
 
-def lane_col(mat, pos):
-    return jnp.broadcast_to(mat[:, pos:pos + 1], mat.shape)
-
-
-def factor_loop(gram, work, rmat):
+def split3(mat):
+    hi = mat.astype(jnp.bfloat16)
+    rest = mat - hi.astype(jnp.float32)
+    mid = rest.astype(jnp.bfloat16)
+    lo = (rest - mid.astype(jnp.float32)).astype(jnp.bfloat16)
+    return hi, mid, lo
+
+
+def factor_loop(gram, work, rmat, between):
     lanes = lax.broadcasted_iota(jnp.int32, (1, NPAN), 1)
     for panel in range(PANELS):
         base = panel * WIDTH
@@ -57,6 +61,7 @@
             return carry
 
         lax.fori_loop(base, base + WIDTH, step, 0)
+        between(panel)
 
 
 def upper_inverse(mat):
@@ -71,13 +76,255 @@
         size *= 2
     return inv
 
-
-def factor_kernel(pay_ref, xt_ref, top_ref, t_ref, tau_ref, gram, work, rmat):
-    nloc = xt_ref.shape[0]
-    col = lax.axis_index('col')
-    gram[...] = pay_ref[nloc:nloc + NPAN, :]
-    work[...] = pay_ref[2 * nloc + NPAN:, :]
-    factor_loop(gram, work, rmat)
+COLS = 4
+ROWS = 4
+QUARTERS = 4
+MESH = pl.DeviceIdType.MESH
+
+
+def panel_kernel(b_hbm, p_hbm, xt_ref, fix_ref, own_ref, t_ref, tau_ref,
+                 bf32, bhi, bmid, blo, pbuf, hacc, hslot, gslot, sslot, ptop, atop, gram, work, rmat,
+                 own_sem, load_sem, out_sem, chunk_recv, chunk_send, ptop_recv, ptop_send, atop_recv, atop_send,
+                 g_recv, g_send, s_recv, s_send, h_recv, h_send):
+    nloc, nrow = bf32.shape
+    half = nrow // 2
+    quarter = nrow // QUARTERS
+    nload = load_sem.shape[0]
+    lwidth = nrow // nload
+    z = lax.axis_index('col')
+    row = lax.axis_index('row')
+    side = z // 2
+    step_z = 1 - 2 * side
+    is_end = (z == 0) | (z == COLS - 1)
+    is_mid = jnp.logical_not(is_end)
+    others = [(dz, dr) for dz in range(COLS) for dr in range(ROWS) if dz or dr]
+
+    def peer(dz, dr):
+        return {'col': lax.rem(z + dz, COLS), 'row': lax.rem(row + dr, ROWS)}
+
+    own_base = pl.multiple_of(z * WIDTH, WIDTH)
+    own_copy = pltpu.make_async_copy(b_hbm.at[pl.ds(0, WIDTH), :], pbuf.at[pl.ds(own_base, WIDTH), :], own_sem)
+    own_copy.start()
+
+    def load(i):
+        lanes = pl.ds(i * lwidth, lwidth)
+        return pltpu.make_async_copy(b_hbm.at[:, lanes], bf32.at[:, lanes], load_sem.at[i])
+
+    for i in range(nload):
+        load(i).start()
+
+    barrier = pltpu.get_barrier_semaphore()
+    for dz, dr in others:
+        pl.semaphore_signal(barrier, inc=1, device_id=peer(dz, dr), device_id_type=MESH)
+    pl.semaphore_wait(barrier, len(others))
+
+    def chunk(panel, part, direction):
+        pan = panel * step_z + (COLS - 1) * side
+        h, q = divmod(part, 2)
+        par = 2 * (h + side - 2 * h * side) + q
+        rows = pl.ds(pl.multiple_of(pan * WIDTH, WIDTH), WIDTH)
+        lanes = pl.ds(pl.multiple_of(par * quarter, quarter), quarter)
+        view = pbuf.at[rows, lanes]
+        to = z + (step_z if direction else -step_z)
+        return pltpu.make_async_remote_copy(
+            view, view, chunk_send.at[direction, pan, par], chunk_recv.at[pan, par],
+            device_id={'col': lax.rem(to + COLS, COLS)}, device_id_type=MESH)
+
+    def send(panel, parts, direction):
+        for part in parts:
+            chunk(panel, part, direction).start()
+
+    def arrive(panel, parts):
+        for part in parts:
+            chunk(panel, part, 0).wait_recv()
+
+    own_copy.wait()
+    view = pbuf.at[pl.ds(own_base, WIDTH), pl.ds(0, NPAN)]
+
+    def ptop_copy(zz, dz, dr, idx):
+        rows = pl.ds(pl.multiple_of(zz * WIDTH, WIDTH), WIDTH)
+        return pltpu.make_async_remote_copy(
+            pbuf.at[rows, pl.ds(0, NPAN)], ptop.at[rows, :], ptop_send.at[idx], ptop_recv.at[zz],
+            device_id=peer(dz, dr), device_id_type=MESH)
+
+    @pl.when(row == 0)
+    def _():
+        for idx, (dz, dr) in enumerate(others):
+            ptop_copy(z, dz, dr, idx).start()
+
+    @pl.when(is_end)
+    def _():
+        send(0, (2, 3, 0, 1), 1)
+
+    @pl.when(is_mid)
+    def _():
+        send(1, (2, 3), 1)
+        send(1, (0, 1, 2, 3), 0)
+
+    def atop_copy(dr):
+        return pltpu.make_async_remote_copy(
+            bf32.at[:, pl.ds(0, NPAN)], atop, atop_send.at[dr - 1], atop_recv,
+            device_id=peer(0, dr), device_id_type=MESH)
+
+    def split_step(i, carry):
+        lanes = pl.ds(pl.multiple_of(i * lwidth, lwidth), lwidth)
+        pltpu.make_async_copy(b_hbm.at[:, lanes], bf32.at[:, lanes], load_sem.at[i]).wait()
+        hi, mid, lo = split3(bf32[:, lanes])
+        bhi[:, lanes] = hi
+        bmid[:, lanes] = mid
+        blo[:, lanes] = lo
+        return carry
+
+    split_step(0, 0)
+
+    @pl.when(row == 0)
+    def _():
+        for dr in range(1, ROWS):
+            atop_copy(dr).start()
+        ptop[pl.ds(own_base, WIDTH), :] = pbuf[pl.ds(own_base, WIDTH), :NPAN]
+        atop[...] = bf32[:, :NPAN]
+
+    lax.fori_loop(1, nload, split_step, 0)
+
+    def h_job(base, count, h_idx, first):
+        kc = half // 2
+        rows = pl.ds(pl.multiple_of(base, WIDTH), count)
+        for sub in range(2):
+            lanes = pl.ds(pl.multiple_of(h_idx * half + sub * kc, kc), kc)
+            phi, pmid, plo = split3(pbuf[rows, lanes])
+            cat = jnp.concatenate([phi, pmid, plo], axis=0)
+            mm = lambda left, right: lax.dot_general(left, right, NT, preferred_element_type=jnp.float32)
+            low = mm(blo[:, lanes], phi)
+            middle = mm(bmid[:, lanes], cat[:2 * count])
+            high = mm(bhi[:, lanes], cat)
+            high, middle, low = high.T, middle.T, low.T
+            tot = low + middle[count:2 * count] + high[2 * count:]
+            tot = tot + middle[:count] + high[count:2 * count]
+            tot = tot + high[:count]
+            if first and sub == 0:
+                hacc[rows, :] = tot
+            else:
+                hacc[rows, :] += tot
+
+    def h_rows(piece):
+        if piece == 0:
+            return pl.multiple_of(2 * WIDTH * side, WIDTH), 2 * WIDTH
+        pan = (piece + 1) * step_z + (COLS - 1) * side
+        return pl.multiple_of(pan * WIDTH, WIDTH), WIDTH
+
+    def h_copy(piece, dr):
+        base, count = h_rows(piece)
+        rows = pl.ds(base, count)
+        return pltpu.make_async_remote_copy(
+            hacc.at[rows, :], hslot.at[3 - dr, rows, :], h_send.at[piece, dr - 1], h_recv.at[piece, 3 - dr],
+            device_id=peer(0, dr), device_id_type=MESH)
+
+    def h_start(piece):
+        for dr in range(1, ROWS):
+            h_copy(piece, dr).start()
+
+    def g_copy(dr):
+        return pltpu.make_async_remote_copy(
+            gslot.at[row], gslot.at[row], g_send.at[dr - 1], g_recv.at[row],
+            device_id=peer(0, dr), device_id_type=MESH)
+
+    def g_wait(dr):
+        src = lax.rem(row + dr, ROWS)
+        pltpu.make_async_remote_copy(
+            gslot.at[src], gslot.at[src], g_send.at[dr - 1], g_recv.at[src],
+            device_id=peer(0, dr), device_id_type=MESH).wait_recv()
+
+    def s_copy(idx, dz):
+        return pltpu.make_async_remote_copy(
+            sslot.at[idx], sslot.at[idx], s_send.at[dz - 1], s_recv.at[idx],
+            device_id=peer(dz, 0), device_id_type=MESH)
+
+    near = 2 * WIDTH * side
+    far = 2 * WIDTH - near
+
+    @pl.when(is_mid)
+    def _():
+        arrive(0, (2,))
+        send(0, (2,), 1)
+        arrive(2, (0,))
+        send(2, (0,), 0)
+        arrive(0, (3,))
+        send(0, (3,), 1)
+        send(1, (0, 1), 1)
+        arrive(2, (1,))
+        send(2, (1,), 0)
+
+    @pl.when(is_end)
+    def _():
+        arrive(1, (0, 1))
+
+    half_a = side
+    half_b = 1 - side
+    first_half = jnp.where(is_end, half_a, half_b)
+    h_job(near, 2 * WIDTH, first_half, True)
+
+    @pl.when(is_mid)
+    def _():
+        arrive(3, (0,))
+        send(3, (0,), 0)
+        arrive(0, (0,))
+        send(0, (0,), 1)
+        arrive(0, (1,))
+        send(0, (1,), 1)
+        arrive(3, (1,))
+        pan = pbuf[:, pl.ds(pl.multiple_of(half_a * half, half), half)]
+        gslot[row] = dot(pan, pan, NT)
+        for dr in range(1, ROWS):
+            g_copy(dr).start()
+
+    @pl.when(is_end)
+    def _():
+        arrive(1, (2, 3))
+
+    h_job(near, 2 * WIDTH, 1 - first_half, False)
+    h_start(0)
+
+    @pl.when(is_mid)
+    def _():
+        for dr in range(1, ROWS):
+            g_wait(dr)
+        sslot[side] = (gslot[0] + gslot[1]) + (gslot[2] + gslot[3])
+        for dz in range(1, COLS):
+            s_copy(side, dz).start()
+        send(3, (1,), 0)
+        arrive(2, (2, 3))
+        send(2, (2, 3), 0)
+        h_job(far, 2 * WIDTH, half_a, True)
+        s_copy(1 - side, 1).wait_recv()
+
+    @pl.when(is_end)
+    def _():
+        s_copy(0, 1).wait_recv()
+        s_copy(1, 1).wait_recv()
+
+    for zz in range(COLS):
+        @pl.when((row != 0) | (z != zz))
+        def _():
+            ptop_copy(zz, 1, 0, 0).wait_recv()
+
+    gram[...] = sslot[0] + sslot[1]
+    work[...] = ptop[...]
+
+    def between(panel):
+        if panel == 1:
+            @pl.when(is_mid)
+            def _():
+                arrive(3, (2, 3))
+                send(3, (2, 3), 0)
+
+    factor_loop(gram, work, rmat, between)
+
+    @pl.when(is_end)
+    def _():
+        arrive(2, (0, 1))
+        arrive(3, (0, 1))
+        h_job(far, 2 * WIDTH, half_a, True)
+
     rows = lax.broadcasted_iota(jnp.int32, (NPAN, NPAN), 0)
     cols = lax.broadcasted_iota(jnp.int32, (NPAN, NPAN), 1)
     done = work[...]
@@ -91,31 +338,89 @@
         base = panel * WIDTH
         t_ref[panel] = tmat[base:base + WIDTH, base:base + WIDTH]
     tau_ref[...] = jnp.sum(jnp.where(cols == rows, tmat, 0.0), axis=0, keepdims=True)
-    h_t = pay_ref[:nloc, :]
-    top_t = pay_ref[nloc + NPAN:2 * nloc + NPAN, :]
-    pan_t = pay_ref[2 * nloc + NPAN:, :]
-    m1 = dot(v1t, tmat, TN)
-    m2 = dot(cst, tmat, TN)
-    k1 = m1 - dot(pan_t, m2, TN)
-    yt = dot(top_t, k1) + dot(h_t, m2)
-    xt_ref[...] = dot(yt, cst)
-    top_ref[...] = top_t - dot(yt, v1t)
-    final = jnp.where(cols > rows, done, 0.0) + rfac.T
-    work[...] = final
-    gram[...] = -cst
-    base = pl.multiple_of(col * WIDTH, WIDTH)
-    xt_ref[:WIDTH, :] = gram[pl.ds(base, WIDTH), :]
-    top_ref[:WIDTH, :] = work[pl.ds(base, WIDTH), :]
-
-
-def update_kernel(b_ref, p_ref, xt_ref, top_ref, out_ref):
-    prod = dot(xt_ref[...], p_ref[...])
+    rt = rfac.T
+    fix_ref[...] = ptop[...] - rt
+    work[...] = jnp.where(cols > rows, done, 0.0) + rt
+    own_ref[...] = work[pl.ds(own_base, WIDTH), :]
+    nmat = dot(cst, dot(tmat, cst, (((0,), (0,)), ((), ()))), (((0,), (0,)), ((), ())))
+    gram[...] = nmat
+    work[...] = cst
+
+    @pl.when(is_end)
+    def _():
+        arrive(2, (2, 3))
+
+    @pl.when(row != 0)
+    def _():
+        atop_copy(1).wait_recv()
+
+    base2, _ = h_rows(1)
+    h_job(base2, WIDTH, half_b, False)
+    h_start(1)
+
+    @pl.when(is_end)
+    def _():
+        arrive(3, (2, 3))
+
+    out_copy = pltpu.make_async_copy(pbuf, p_hbm, out_sem)
+    out_copy.start()
+    base3, _ = h_rows(2)
+    h_job(base3, WIDTH, half_b, False)
+    h_start(2)
+    corr = lax.dot_general(rfac, atop[...], (((0,), (1,)), ((), ())), precision=HIGHEST, preferred_element_type=jnp.float32)
+    for piece in range(3):
+        for dr in range(1, ROWS):
+            h_copy(piece, dr).wait()
+    total = (hacc[...] - corr) + (hslot[0] + hslot[1] + hslot[2])
+    xt_ref[...] = lax.dot_general(total, gram[...], (((0,), (1,)), ((), ())), precision=HIGHEST, preferred_element_type=jnp.float32)
+    xt_ref[:WIDTH, :] = -work[pl.ds(own_base, WIDTH), :]
+    out_copy.wait()
+
+    def sent(panel, parts, direction):
+        for part in parts:
+            chunk(panel, part, direction).wait_send()
+
+    @pl.when(is_end)
+    def _():
+        sent(0, (0, 1, 2, 3), 1)
+
+    @pl.when(is_mid)
+    def _():
+        for panel in (0, 1):
+            sent(panel, (0, 1, 2, 3), 1)
+        for panel in (1, 2, 3):
+            sent(panel, (0, 1, 2, 3), 0)
+        for dr in range(1, ROWS):
+            g_copy(dr).wait_send()
+        for dz in range(1, COLS):
+            s_copy(side, dz).wait_send()
+
+    @pl.when(row == 0)
+    def _():
+        for idx, (dz, dr) in enumerate(others):
+            ptop_copy(z, dz, dr, idx).wait_send()
+        for dr in range(1, ROWS):
+            atop_copy(dr).wait_send()
+
+
+def update_kernel(b_ref, p_ref, xt_ref, fix_ref, own_ref, out_ref, xcat):
+    @pl.when(pl.program_id(0) == 0)
+    def _():
+        hi, mid, lo = split3(xt_ref[...])
+        for slot, part in enumerate((hi, hi, hi, mid, mid, lo)):
+            xcat[:, slot * NPAN:(slot + 1) * NPAN] = part
+
+    hi, mid, lo = split3(p_ref[...])
+    pcat = jnp.concatenate([hi, mid, lo, hi, mid, hi], axis=0)
+    prod = lax.dot_general(xcat[...], pcat, NN, preferred_element_type=jnp.float32)
     out_ref[:WIDTH, :] = -prod[:WIDTH, :]
     out_ref[WIDTH:, :] = b_ref[WIDTH:, :] - prod[WIDTH:, :]
 
     @pl.when((lax.axis_index('row') == 0) & (pl.program_id(0) == 0))
     def _():
-        out_ref[:, :NPAN] = top_ref[...]
+        top = dot(xt_ref[...], fix_ref[...])
+        out_ref[:WIDTH, :NPAN] = own_ref[...]
+        out_ref[WIDTH:, :NPAN] = b_ref[WIDTH:, :NPAN] - top[WIDTH:, :]
 
 
 def solution(mesh):
@@ -125,20 +430,28 @@
         nrow, nblk, width = a_local.shape
         nloc = nblk * width
         b_t = a_local.transpose(1, 2, 0).reshape(nloc, nrow)
-        row = lax.axis_index('row')
-        p_t = lax.all_gather(b_t[:width], 'col', axis=0, tiled=True)
-        h_t = dot(b_t, p_t, NT)
-        g_t = dot(p_t, p_t, NT)
-        tops = jnp.concatenate([b_t[:, :NPAN], p_t[:, :NPAN]], axis=0)
-        tops = jnp.where(row == 0, tops, 0.0)
-        pay = lax.psum(jnp.concatenate([h_t, g_t, tops], axis=0), 'row')
         full = lambda shape: jax.ShapeDtypeStruct(shape, jnp.float32)
-        xt, top, tfac, tau = pl.pallas_call(
-            factor_kernel,
-            out_shape=(full((nloc, NPAN)), full((nloc, NPAN)), full((PANELS, WIDTH, WIDTH)), full((1, NPAN))),
-            scratch_shapes=[pltpu.VMEM((NPAN, NPAN), jnp.float32)] * 3,
-            name='factor',
-        )(pay)
+        vmem = pl.BlockSpec(memory_space=pltpu.VMEM)
+        hbm = pl.BlockSpec(memory_space=pl.ANY)
+        buf = lambda *shape: pltpu.VMEM(shape, jnp.float32)
+        dma = lambda *shape: pltpu.SemaphoreType.DMA(shape)
+        bf16 = pltpu.VMEM((nloc, nrow), jnp.bfloat16)
+        p_t, xt, fix, own, tfac, tau = pl.pallas_call(
+            panel_kernel,
+            in_specs=[hbm],
+            out_specs=(hbm, vmem, vmem, vmem, vmem, vmem),
+            out_shape=(full((NPAN, nrow)), full((nloc, NPAN)), full((NPAN, NPAN)), full((WIDTH, NPAN)), full((PANELS, WIDTH, WIDTH)), full((1, NPAN))),
+            scratch_shapes=[
+                buf(nloc, nrow), bf16, bf16, bf16, buf(NPAN, nrow), buf(NPAN, nloc), buf(3, NPAN, nloc),
+                buf(ROWS, NPAN, NPAN), buf(2, NPAN, NPAN), buf(NPAN, NPAN), buf(nloc, NPAN),
+                buf(NPAN, NPAN), buf(NPAN, NPAN), buf(NPAN, NPAN),
+                pltpu.SemaphoreType.DMA, dma(12), pltpu.SemaphoreType.DMA,
+                dma(COLS, QUARTERS), dma(2, COLS, QUARTERS), dma(COLS), dma(COLS * ROWS - 1), pltpu.SemaphoreType.DMA, dma(ROWS - 1),
+                dma(ROWS), dma(ROWS - 1), dma(2), dma(COLS - 1), dma(3, 3), dma(3, 3),
+            ],
+            compiler_params=pltpu.CompilerParams(collective_id=0, has_side_effects=True, vmem_limit_bytes=60 * 1024 * 1024),
+            name='panels',
+        )(b_t)
         chunk = 512
         out = pl.pallas_call(
             update_kernel,
@@ -147,12 +460,14 @@
                 pl.BlockSpec((nloc, chunk), lambda i: (0, i)),
                 pl.BlockSpec((NPAN, chunk), lambda i: (0, i)),
                 pl.BlockSpec((nloc, NPAN), lambda i: (0, 0)),
-                pl.BlockSpec((nloc, NPAN), lambda i: (0, 0)),
+                pl.BlockSpec((NPAN, NPAN), lambda i: (0, 0)),
+                pl.BlockSpec((WIDTH, NPAN), lambda i: (0, 0)),
             ],
             out_specs=pl.BlockSpec((nloc, chunk), lambda i: (0, i)),
             out_shape=full((nloc, nrow)),
+            scratch_shapes=[pltpu.VMEM((nloc, 6 * NPAN), jnp.bfloat16)],
             name='update',
-        )(b_t, p_t, xt, top)
+        )(b_t, p_t, xt, fix, own)
         return out.reshape(nblk, width, nrow).transpose(2, 0, 1), tau.reshape(NPAN), tfac
 
     return jax.shard_map(device_fn, mesh=mesh, in_specs=(block_spec,), out_specs=(block_spec, P('batch'), P('batch', None, None)), check_vma=False)

time: 176 us -> 99.7 us (0.57)
  the two profiles are of different devices: /device:TPU:1 before, /device:TPU:0 now
where the time goes in v2:
time: 99.7 us; the launch traced here: 99.3 us
  Pallas kernels  97.5 us (98%)
  local copies, waits for them, and re-layouts  1.15 us (1%)
    pallas_call x1, Pallas kernels, device_fn(): pl.pallas_call(panel_kernel, in_specs=[hbm], out_specs=(hbm, vmem, vmem,...  80.3 us
    pallas_call x1, Pallas kernels, device_fn(): pl.pallas_call(update_kernel, grid=(nrow // chunk,), in_specs=[pl.BlockSp...  17.2 us

profile of v2, /device:TPU:0, one launch (start us, length us, event | category | flops | bytes accessed | tf_op | source)
XLA Modules:
  0.0 99.3 jit_solution(17590228629482290484)
XLA Ops:
  0.6 80.3 %panels.1 = (f32[128,6144]{1,0:T(8,128)}, f32[512,128]{1,0:T(8,128)}, f32[128,128]{1,0:T(8,128)}, f32[32,128]{1,0:T(8,128)}, f32[4,32,32]{2,1,0:T(8,128)}, /*index=5*/f32[1,128]{1,0:T(1,128)}) custom-call(f32[512,6144]{1,0:T(8,128)} %bitcast.7), custom_call_target="tpu_custom_call" | custom-call | tf_op jit(solution)/shard_map/panels/pallas_call | solution.py:439
  80.9 0.0 copy-start.1
  80.9 0.0 copy-start
  80.9 17.2 %update.1 = f32[512,6144]{1,0:T(8,128)} custom-call(f32[512,6144]{1,0:T(8,128)} %bitcast.8, f32[128,6144]{1,0:T(8,128)} %get-tuple-element.9.p_ref, f32[512,128]{1,0:T(8,128)} %get-tuple-element.10.xt_ref, f32[128,128]{1,0:T(8,128)} %get-tuple-element.11.fix_ref, f32[32,128]{1,0:T(8,128)} %get-tuple-element.12.own_ref), custom_call_target="tpu_custom_call" | custom-call | tf_op jit(solution)/shard_map/update/pallas_call | solution.py:456
  98.2 0.0 copy-done.1
  98.2 0.5 copy.6
  98.7 0.0 copy-done
  98.7 0.6 copy.7
Async XLA Ops:
  80.9 17.3 %copy-start.1 = (f32[1,128]{1,0:T(1,128)S(1)}, f32[1,128]{1,0:T(1,128)}, u32[]{:S(2)}) copy-start(f32[1,128]{1,0:T(1,128)} %get-tuple-element.13) | copy-start | bytes 1540
  80.9 17.8 %copy-start = (f32[4,32,32]{2,1,0:T(8,128)S(1)}, f32[4,32,32]{2,1,0:T(8,128)}, u32[]{:S(2)}) copy-start(f32[4,32,32]{2,1,0:T(8,128)} %get-tuple-element.20) | copy-start | bytes 49156

commit v3 on v2

--- a/solution.py
+++ b/solution.py
@@ -84,7 +84,7 @@
 
 def panel_kernel(b_hbm, p_hbm, xt_ref, fix_ref, own_ref, t_ref, tau_ref,
                  bf32, bhi, bmid, blo, pbuf, hacc, hslot, gslot, sslot, ptop, atop, gram, work, rmat,
-                 own_sem, load_sem, out_sem, chunk_recv, chunk_send, ptop_recv, ptop_send, atop_recv, atop_send,
+                 own_sem, load_sem, out_sem, chunk_recv, chunk_send, ptop_recv, ptop_send, tops_recv, tops_send, atop_recv, atop_send,
                  g_recv, g_send, s_recv, s_send, h_recv, h_send):
     nloc, nrow = bf32.shape
     half = nrow // 2
@@ -97,7 +97,7 @@
     step_z = 1 - 2 * side
     is_end = (z == 0) | (z == COLS - 1)
     is_mid = jnp.logical_not(is_end)
-    others = [(dz, dr) for dz in range(COLS) for dr in range(ROWS) if dz or dr]
+    others = [(dz, 0) for dz in range(1, COLS)] + [(0, dr) for dr in range(1, ROWS)]
 
     def peer(dz, dr):
         return {'col': lax.rem(z + dz, COLS), 'row': lax.rem(row + dr, ROWS)}
@@ -139,18 +139,22 @@
             chunk(panel, part, 0).wait_recv()
 
     own_copy.wait()
-    view = pbuf.at[pl.ds(own_base, WIDTH), pl.ds(0, NPAN)]
-
-    def ptop_copy(zz, dz, dr, idx):
+
+    def ptop_copy(zz, dz):
         rows = pl.ds(pl.multiple_of(zz * WIDTH, WIDTH), WIDTH)
         return pltpu.make_async_remote_copy(
-            pbuf.at[rows, pl.ds(0, NPAN)], ptop.at[rows, :], ptop_send.at[idx], ptop_recv.at[zz],
-            device_id=peer(dz, dr), device_id_type=MESH)
+            pbuf.at[rows, pl.ds(0, NPAN)], ptop.at[rows, :], ptop_send.at[dz - 1], ptop_recv.at[zz],
+            device_id=peer(dz, 0), device_id_type=MESH)
+
+    def tops_copy(dr):
+        return pltpu.make_async_remote_copy(
+            ptop, ptop, tops_send.at[dr - 1], tops_recv,
+            device_id=peer(0, dr), device_id_type=MESH)
 
     @pl.when(row == 0)
     def _():
-        for idx, (dz, dr) in enumerate(others):
-            ptop_copy(z, dz, dr, idx).start()
+        for dz in range(1, COLS):
+            ptop_copy(z, dz).start()
 
     @pl.when(is_end)
     def _():
@@ -185,6 +189,13 @@
         atop[...] = bf32[:, :NPAN]
 
     lax.fori_loop(1, nload, split_step, 0)
+
+    @pl.when(row == 0)
+    def _():
+        for dz in range(1, COLS):
+            ptop_copy(lax.rem(z + dz, COLS), dz).wait_recv()
+        for dr in range(1, ROWS):
+            tops_copy(dr).start()
 
     def h_job(base, count, h_idx, first):
         kc = half // 2
@@ -265,15 +276,17 @@
 
     @pl.when(is_mid)
     def _():
-        arrive(3, (0,))
-        send(3, (0,), 0)
-        arrive(0, (0,))
-        send(0, (0,), 1)
-        arrive(0, (1,))
-        send(0, (1,), 1)
-        arrive(3, (1,))
-        pan = pbuf[:, pl.ds(pl.multiple_of(half_a * half, half), half)]
-        gslot[row] = dot(pan, pan, NT)
+        for q in range(2):
+            arrive(3, (q,))
+            arrive(0, (q,))
+            phi, pmid, plo = split3(pbuf[:, pl.ds(pl.multiple_of(half_a * half + q * quarter, quarter), quarter)])
+            cat = jnp.concatenate([phi, pmid, plo], axis=0)
+            mm = lambda left, right: lax.dot_general(left, right, NT, preferred_element_type=jnp.float32)
+            high, middle, low = mm(phi, cat), mm(pmid, cat[:2 * NPAN]), mm(plo, phi)
+            tot = low + middle[:, NPAN:] + high[:, 2 * NPAN:]
+            tot = tot + middle[:, :NPAN] + high[:, NPAN:2 * NPAN]
+            tot = tot + high[:, :NPAN]
+            gslot[row] = tot if q == 0 else gslot[row] + tot
         for dr in range(1, ROWS):
             g_copy(dr).start()
 
@@ -291,27 +304,32 @@
         sslot[side] = (gslot[0] + gslot[1]) + (gslot[2] + gslot[3])
         for dz in range(1, COLS):
             s_copy(side, dz).start()
-        send(3, (1,), 0)
+        send(3, (0, 1), 0)
+        send(0, (0, 1), 1)
         arrive(2, (2, 3))
         send(2, (2, 3), 0)
         h_job(far, 2 * WIDTH, half_a, True)
         s_copy(1 - side, 1).wait_recv()
 
-    @pl.when(is_end)
-    def _():
+    base2, _ = h_rows(1)
+    base3, _ = h_rows(2)
+
+    @pl.when(is_end)
+    def _():
+        arrive(2, (0, 1))
+        h_job(base2, WIDTH, half_a, True)
         s_copy(0, 1).wait_recv()
         s_copy(1, 1).wait_recv()
 
-    for zz in range(COLS):
-        @pl.when((row != 0) | (z != zz))
-        def _():
-            ptop_copy(zz, 1, 0, 0).wait_recv()
+    @pl.when(row != 0)
+    def _():
+        tops_copy(1).wait_recv()
 
     gram[...] = sslot[0] + sslot[1]
     work[...] = ptop[...]
 
     def between(panel):
-        if panel == 1:
+        if panel == 2:
             @pl.when(is_mid)
             def _():
                 arrive(3, (2, 3))
@@ -321,10 +339,12 @@
 
     @pl.when(is_end)
     def _():
-        arrive(2, (0, 1))
         arrive(3, (0, 1))
-        h_job(far, 2 * WIDTH, half_a, True)
-
+        h_job(base3, WIDTH, half_a, True)
+        arrive(2, (2, 3))
+
+    h_job(base2, WIDTH, half_b, False)
+    h_start(1)
     rows = lax.broadcasted_iota(jnp.int32, (NPAN, NPAN), 0)
     cols = lax.broadcasted_iota(jnp.int32, (NPAN, NPAN), 1)
     done = work[...]
@@ -334,6 +354,14 @@
     tinv = -dot(dot(v1t, rfac), cst, NT)
     tinv = jnp.where(cols >= rows, tinv, 0.0)
     tmat = upper_inverse(tinv)
+    @pl.when(is_end)
+    def _():
+        arrive(3, (2, 3))
+
+    out_copy = pltpu.make_async_copy(pbuf, p_hbm, out_sem)
+    out_copy.start()
+    h_job(base3, WIDTH, half_b, False)
+    h_start(2)
     for panel in range(PANELS):
         base = panel * WIDTH
         t_ref[panel] = tmat[base:base + WIDTH, base:base + WIDTH]
@@ -346,27 +374,11 @@
     gram[...] = nmat
     work[...] = cst
 
-    @pl.when(is_end)
-    def _():
-        arrive(2, (2, 3))
 
     @pl.when(row != 0)
     def _():
         atop_copy(1).wait_recv()
 
-    base2, _ = h_rows(1)
-    h_job(base2, WIDTH, half_b, False)
-    h_start(1)
-
-    @pl.when(is_end)
-    def _():
-        arrive(3, (2, 3))
-
-    out_copy = pltpu.make_async_copy(pbuf, p_hbm, out_sem)
-    out_copy.start()
-    base3, _ = h_rows(2)
-    h_job(base3, WIDTH, half_b, False)
-    h_start(2)
     corr = lax.dot_general(rfac, atop[...], (((0,), (1,)), ((), ())), precision=HIGHEST, preferred_element_type=jnp.float32)
     for piece in range(3):
         for dr in range(1, ROWS):
@@ -397,30 +409,63 @@
 
     @pl.when(row == 0)
     def _():
-        for idx, (dz, dr) in enumerate(others):
-            ptop_copy(z, dz, dr, idx).wait_send()
+        for dz in range(1, COLS):
+            ptop_copy(z, dz).wait_send()
         for dr in range(1, ROWS):
             atop_copy(dr).wait_send()
-
-
-def update_kernel(b_ref, p_ref, xt_ref, fix_ref, own_ref, out_ref, xcat):
-    @pl.when(pl.program_id(0) == 0)
-    def _():
-        hi, mid, lo = split3(xt_ref[...])
-        for slot, part in enumerate((hi, hi, hi, mid, mid, lo)):
-            xcat[:, slot * NPAN:(slot + 1) * NPAN] = part
-
-    hi, mid, lo = split3(p_ref[...])
-    pcat = jnp.concatenate([hi, mid, lo, hi, mid, hi], axis=0)
-    prod = lax.dot_general(xcat[...], pcat, NN, preferred_element_type=jnp.float32)
-    out_ref[:WIDTH, :] = -prod[:WIDTH, :]
-    out_ref[WIDTH:, :] = b_ref[WIDTH:, :] - prod[WIDTH:, :]
-
-    @pl.when((lax.axis_index('row') == 0) & (pl.program_id(0) == 0))
-    def _():
-        top = dot(xt_ref[...], fix_ref[...])
-        out_ref[:WIDTH, :NPAN] = own_ref[...]
-        out_ref[WIDTH:, :NPAN] = b_ref[WIDTH:, :NPAN] - top[WIDTH:, :]
+            tops_copy(dr).wait_send()
+
+
+def update_kernel(b_hbm, p_hbm, xt_ref, fix_ref, own_ref, tfac_ref, tau_in, out_hbm, t_ref, tau_ref, bbuf, pbuf, xcat, b_sem, p_sem, out_sem):
+    nsteps = b_sem.shape[0]
+    chunk = bbuf.shape[1] // nsteps
+    first = (lax.axis_index('row') == 0)
+
+    def lanes_of(i):
+        return pl.ds(pl.multiple_of(i * chunk, chunk), chunk)
+
+    def loads(i):
+        lanes = lanes_of(i)
+        return (pltpu.make_async_copy(p_hbm.at[:, lanes], pbuf.at[:, lanes], p_sem.at[i]),
+                pltpu.make_async_copy(b_hbm.at[:, lanes], bbuf.at[:, lanes], b_sem.at[i]))
+
+    def store(i):
+        lanes = lanes_of(i)
+        return pltpu.make_async_copy(bbuf.at[:, lanes], out_hbm.at[:, lanes], out_sem.at[i])
+
+    for i in range(nsteps):
+        for copy in loads(i):
+            copy.start()
+    t_ref[...] = tfac_ref[...]
+    tau_ref[...] = tau_in[...]
+    hi, mid, lo = split3(xt_ref[...])
+    for slot, part in enumerate((hi, hi, hi, mid, mid, lo)):
+        xcat[:, slot * NPAN:(slot + 1) * NPAN] = part
+    top = dot(xt_ref[...], fix_ref[...])
+
+    def step(i, carry):
+        for copy in loads(i):
+            copy.wait()
+        lanes = lanes_of(i)
+        hi, mid, lo = split3(pbuf[:, lanes])
+        pcat = jnp.concatenate([hi, mid, lo, hi, mid, hi], axis=0)
+        prod = lax.dot_general(xcat[...], pcat, NN, preferred_element_type=jnp.float32)
+        use_top = first & (i == 0)
+        head = prod[:, :NPAN]
+        block = bbuf[:, lanes]
+        new_own = jnp.where(use_top, own_ref[...], -head[:WIDTH])
+        new_top = block[WIDTH:, :NPAN] - jnp.where(use_top, top[WIDTH:], head[WIDTH:])
+        bbuf[:WIDTH, pl.ds(pl.multiple_of(i * chunk, chunk), NPAN)] = new_own
+        bbuf[WIDTH:, pl.ds(pl.multiple_of(i * chunk, chunk), NPAN)] = new_top
+        rest = pl.ds(pl.multiple_of(i * chunk + NPAN, NPAN), chunk - NPAN)
+        bbuf[:WIDTH, rest] = -prod[:WIDTH, NPAN:]
+        bbuf[WIDTH:, rest] = block[WIDTH:, NPAN:] - prod[WIDTH:, NPAN:]
+        store(i).start()
+        return carry
+
+    lax.fori_loop(0, nsteps, step, 0)
+    for i in range(nsteps):
+        store(i).wait()
 
 
 def solution(mesh):
@@ -446,28 +491,21 @@
                 buf(ROWS, NPAN, NPAN), buf(2, NPAN, NPAN), buf(NPAN, NPAN), buf(nloc, NPAN),
                 buf(NPAN, NPAN), buf(NPAN, NPAN), buf(NPAN, NPAN),
                 pltpu.SemaphoreType.DMA, dma(12), pltpu.SemaphoreType.DMA,
-                dma(COLS, QUARTERS), dma(2, COLS, QUARTERS), dma(COLS), dma(COLS * ROWS - 1), pltpu.SemaphoreType.DMA, dma(ROWS - 1),
+                dma(COLS, QUARTERS), dma(2, COLS, QUARTERS), dma(COLS), dma(COLS - 1), pltpu.SemaphoreType.DMA, dma(ROWS - 1), pltpu.SemaphoreType.DMA, dma(ROWS - 1),
                 dma(ROWS), dma(ROWS - 1), dma(2), dma(COLS - 1), dma(3, 3), dma(3, 3),
             ],
             compiler_params=pltpu.CompilerParams(collective_id=0, has_side_effects=True, vmem_limit_bytes=60 * 1024 * 1024),
             name='panels',
         )(b_t)
-        chunk = 512
-        out = pl.pallas_call(
+        steps = 8
+        out, tfac, tau = pl.pallas_call(
             update_kernel,
-            grid=(nrow // chunk,),
-            in_specs=[
-                pl.BlockSpec((nloc, chunk), lambda i: (0, i)),
-                pl.BlockSpec((NPAN, chunk), lambda i: (0, i)),
-                pl.BlockSpec((nloc, NPAN), lambda i: (0, 0)),
-                pl.BlockSpec((NPAN, NPAN), lambda i: (0, 0)),
-                pl.BlockSpec((WIDTH, NPAN), lambda i: (0, 0)),
-            ],
-            out_specs=pl.BlockSpec((nloc, chunk), lambda i: (0, i)),
-            out_shape=full((nloc, nrow)),
-            scratch_shapes=[pltpu.VMEM((nloc, 6 * NPAN), jnp.bfloat16)],
+            in_specs=[hbm, hbm, vmem, vmem, vmem, vmem, vmem],
+            out_specs=(hbm, vmem, vmem),
+            out_shape=(full((nloc, nrow)), full((PANELS, WIDTH, WIDTH)), full((1, NPAN))),
+            scratch_shapes=[buf(nloc, nrow), buf(NPAN, nrow), pltpu.VMEM((nloc, 6 * NPAN), jnp.bfloat16), dma(steps), dma(steps), dma(steps)],
             name='update',
-        )(b_t, p_t, xt, fix, own)
+        )(b_t, p_t, xt, fix, own, tfac, tau)
         return out.reshape(nblk, width, nrow).transpose(2, 0, 1), tau.reshape(NPAN), tfac
 
     return jax.shard_map(device_fn, mesh=mesh, in_specs=(block_spec,), out_specs=(block_spec, P('batch'), P('batch', None, None)), check_vma=False)

time: 99.7 us -> 86.1 us (0.86)
  the two profiles are of different devices: /device:TPU:0 before, /device:TPU:1 now
where the time goes in v3:
time: 86.1 us; the launch traced here: 86 us
  Pallas kernels  85.2 us (99%)
    pallas_call x1, Pallas kernels, device_fn(): pl.pallas_call(panel_kernel, in_specs=[hbm], out_specs=(hbm, vmem, vmem,...  72.4 us
    pallas_call x1, Pallas kernels, device_fn(): pl.pallas_call(update_kernel, in_specs=[hbm, hbm, vmem, vmem, vmem, vmem,...  12.8 us

profile of v3, /device:TPU:1, one launch (start us, length us, event | category | flops | bytes accessed | tf_op | source)
XLA Modules:
  0.0 86.0 jit_solution(4680251567267356894)
XLA Ops:
  0.6 72.4 %panels.1 = (f32[128,6144]{1,0:T(8,128)}, f32[512,128]{1,0:T(8,128)}, f32[128,128]{1,0:T(8,128)}, f32[32,128]{1,0:T(8,128)}, f32[4,32,32]{2,1,0:T(8,128)}, /*index=5*/f32[1,128]{1,0:T(1,128)}) custom-call(f32[512,6144]{1,0:T(8,128)} %bitcast.7), custom_call_target="tpu_custom_call" | custom-call | tf_op jit(solution)/shard_map/panels/pallas_call | solution.py:484
  73.1 12.8 %update.1 = (f32[512,6144]{1,0:T(8,128)}, f32[4,32,32]{2,1,0:T(8,128)}, f32[1,128]{1,0:T(1,128)}) custom-call(f32[512,6144]{1,0:T(8,128)} %bitcast.8, f32[128,6144]{1,0:T(8,128)} %get-tuple-element.12.p_hbm, f32[512,128]{1,0:T(8,128)} %get-tuple-element.13.xt_ref, f32[128,128]{1,0:T(8,128)} %get-tuple-element.14.fix_ref, ...), custom_call_target="tpu_custom_call" | custom-call | tf_op jit(solution)/shard_map/update/pallas_call | solution.py:501

commit v4 on v3

--- a/solution.py
+++ b/solution.py
@@ -82,10 +82,10 @@
 MESH = pl.DeviceIdType.MESH
 
 
-def panel_kernel(b_hbm, p_hbm, xt_ref, fix_ref, own_ref, t_ref, tau_ref,
-                 bf32, bhi, bmid, blo, pbuf, hacc, hslot, gslot, sslot, ptop, atop, gram, work, rmat,
-                 own_sem, load_sem, out_sem, chunk_recv, chunk_send, ptop_recv, ptop_send, tops_recv, tops_send, atop_recv, atop_send,
-                 g_recv, g_send, s_recv, s_send, h_recv, h_send):
+def panel_kernel(b_hbm, bf32, pbuf, xt_ref, fix_ref, own_ref, t_ref, tau_ref,
+                 bhi, bmid, blo, hacc, hslot, gslot, sslot, ptop, atop, gram, work, rmat,
+                 own_sem, load_sem, chunk_recv, chunk_send, ptop_recv, ptop_send, tops_recv, tops_send, atop_recv, atop_send,
+                 g_recv, g_send, s_recv, s_send, swap_recv, swap_send, h_recv, h_send):
     nloc, nrow = bf32.shape
     half = nrow // 2
     quarter = nrow // QUARTERS
@@ -197,10 +197,12 @@
         for dr in range(1, ROWS):
             tops_copy(dr).start()
 
-    def h_job(base, count, h_idx, first):
+    def h_job(base, count, h_idx, first, before=None):
         kc = half // 2
         rows = pl.ds(pl.multiple_of(base, WIDTH), count)
         for sub in range(2):
+            if before is not None:
+                before(sub)
             lanes = pl.ds(pl.multiple_of(h_idx * half + sub * kc, kc), kc)
             phi, pmid, plo = split3(pbuf[rows, lanes])
             cat = jnp.concatenate([phi, pmid, plo], axis=0)
@@ -245,10 +247,22 @@
             gslot.at[src], gslot.at[src], g_send.at[dr - 1], g_recv.at[src],
             device_id=peer(0, dr), device_id_type=MESH).wait_recv()
 
+    core = lax.rem(row, 2)
+    twin = row + 1 - 2 * core
+    s_rows = pl.ds(pl.multiple_of(core * (NPAN // 2), NPAN // 2), NPAN // 2)
+    t_rows = pl.ds(pl.multiple_of((1 - core) * (NPAN // 2), NPAN // 2), NPAN // 2)
+
     def s_copy(idx, dz):
-        return pltpu.make_async_remote_copy(
-            sslot.at[idx], sslot.at[idx], s_send.at[dz - 1], s_recv.at[idx],
+        view = sslot.at[idx, s_rows, :]
+        return pltpu.make_async_remote_copy(
+            view, view, s_send.at[dz - 1], s_recv.at[idx],
             device_id=peer(dz, 0), device_id_type=MESH)
+
+    def s_swap(idx, view_rows):
+        view = sslot.at[idx, view_rows, :]
+        return pltpu.make_async_remote_copy(
+            view, view, swap_send.at[idx], swap_recv.at[idx],
+            device_id={'row': twin}, device_id_type=MESH)
 
     near = 2 * WIDTH * side
     far = 2 * WIDTH - near
@@ -310,6 +324,8 @@
         send(2, (2, 3), 0)
         h_job(far, 2 * WIDTH, half_a, True)
         s_copy(1 - side, 1).wait_recv()
+        s_swap(1 - side, s_rows).start()
+        s_swap(1 - side, t_rows).wait_recv()
 
     base2, _ = h_rows(1)
     base3, _ = h_rows(2)
@@ -318,8 +334,11 @@
     def _():
         arrive(2, (0, 1))
         h_job(base2, WIDTH, half_a, True)
-        s_copy(0, 1).wait_recv()
-        s_copy(1, 1).wait_recv()
+        for idx in (side, 1 - side):
+            s_copy(idx, 1).wait_recv()
+            s_swap(idx, s_rows).start()
+        for idx in (side, 1 - side):
+            s_swap(idx, t_rows).wait_recv()
 
     @pl.when(row != 0)
     def _():
@@ -354,13 +373,12 @@
     tinv = -dot(dot(v1t, rfac), cst, NT)
     tinv = jnp.where(cols >= rows, tinv, 0.0)
     tmat = upper_inverse(tinv)
-    @pl.when(is_end)
-    def _():
-        arrive(3, (2, 3))
-
-    out_copy = pltpu.make_async_copy(pbuf, p_hbm, out_sem)
-    out_copy.start()
-    h_job(base3, WIDTH, half_b, False)
+    def last_arrival(sub):
+        @pl.when(is_end)
+        def _():
+            arrive(3, (2 + sub,))
+
+    h_job(base3, WIDTH, half_b, False, last_arrival)
     h_start(2)
     for panel in range(PANELS):
         base = panel * WIDTH
@@ -386,7 +404,6 @@
     total = (hacc[...] - corr) + (hslot[0] + hslot[1] + hslot[2])
     xt_ref[...] = lax.dot_general(total, gram[...], (((0,), (1,)), ((), ())), precision=HIGHEST, preferred_element_type=jnp.float32)
     xt_ref[:WIDTH, :] = -work[pl.ds(own_base, WIDTH), :]
-    out_copy.wait()
 
     def sent(panel, parts, direction):
         for part in parts:
@@ -395,6 +412,8 @@
     @pl.when(is_end)
     def _():
         sent(0, (0, 1, 2, 3), 1)
+        for idx in range(2):
+            s_swap(idx, s_rows).wait_send()
 
     @pl.when(is_mid)
     def _():
@@ -406,6 +425,7 @@
             g_copy(dr).wait_send()
         for dz in range(1, COLS):
             s_copy(side, dz).wait_send()
+        s_swap(1 - side, s_rows).wait_send()
 
     @pl.when(row == 0)
     def _():
@@ -416,55 +436,49 @@
             tops_copy(dr).wait_send()
 
 
-def update_kernel(b_hbm, p_hbm, xt_ref, fix_ref, own_ref, tfac_ref, tau_in, out_hbm, t_ref, tau_ref, bbuf, pbuf, xcat, b_sem, p_sem, out_sem):
-    nsteps = b_sem.shape[0]
-    chunk = bbuf.shape[1] // nsteps
-    first = (lax.axis_index('row') == 0)
+def update_kernel(b_ref, p_ref, xt_ref, fix_ref, own_ref, tfac_ref, tau_in, out_hbm, t_ref, tau_ref, obuf, xcat, out_sem):
+    nslots, _, chunk = obuf.shape
+    nsteps = b_ref.shape[1] // chunk
+    first = lax.axis_index('row') == 0
 
     def lanes_of(i):
         return pl.ds(pl.multiple_of(i * chunk, chunk), chunk)
 
-    def loads(i):
-        lanes = lanes_of(i)
-        return (pltpu.make_async_copy(p_hbm.at[:, lanes], pbuf.at[:, lanes], p_sem.at[i]),
-                pltpu.make_async_copy(b_hbm.at[:, lanes], bbuf.at[:, lanes], b_sem.at[i]))
-
     def store(i):
-        lanes = lanes_of(i)
-        return pltpu.make_async_copy(bbuf.at[:, lanes], out_hbm.at[:, lanes], out_sem.at[i])
-
-    for i in range(nsteps):
-        for copy in loads(i):
-            copy.start()
+        slot = lax.rem(i, nslots)
+        return pltpu.make_async_copy(obuf.at[slot], out_hbm.at[:, lanes_of(i)], out_sem.at[slot])
+
     t_ref[...] = tfac_ref[...]
     tau_ref[...] = tau_in[...]
     hi, mid, lo = split3(xt_ref[...])
     for slot, part in enumerate((hi, hi, hi, mid, mid, lo)):
         xcat[:, slot * NPAN:(slot + 1) * NPAN] = part
-    top = dot(xt_ref[...], fix_ref[...])
 
     def step(i, carry):
-        for copy in loads(i):
-            copy.wait()
         lanes = lanes_of(i)
-        hi, mid, lo = split3(pbuf[:, lanes])
+        hi, mid, lo = split3(p_ref[:, lanes])
         pcat = jnp.concatenate([hi, mid, lo, hi, mid, hi], axis=0)
+
+        @pl.when(i >= nslots)
+        def _():
+            store(i - nslots).wait()
+
+        slot = lax.rem(i, nslots)
         prod = lax.dot_general(xcat[...], pcat, NN, preferred_element_type=jnp.float32)
-        use_top = first & (i == 0)
-        head = prod[:, :NPAN]
-        block = bbuf[:, lanes]
-        new_own = jnp.where(use_top, own_ref[...], -head[:WIDTH])
-        new_top = block[WIDTH:, :NPAN] - jnp.where(use_top, top[WIDTH:], head[WIDTH:])
-        bbuf[:WIDTH, pl.ds(pl.multiple_of(i * chunk, chunk), NPAN)] = new_own
-        bbuf[WIDTH:, pl.ds(pl.multiple_of(i * chunk, chunk), NPAN)] = new_top
-        rest = pl.ds(pl.multiple_of(i * chunk + NPAN, NPAN), chunk - NPAN)
-        bbuf[:WIDTH, rest] = -prod[:WIDTH, NPAN:]
-        bbuf[WIDTH:, rest] = block[WIDTH:, NPAN:] - prod[WIDTH:, NPAN:]
+        obuf[slot, :WIDTH, :] = -prod[:WIDTH]
+        obuf[slot, WIDTH:, :] = b_ref[WIDTH:, lanes] - prod[WIDTH:]
+
+        @pl.when(first & (i == 0))
+        def _():
+            top = dot(xt_ref[...], fix_ref[...])
+            obuf[slot, :WIDTH, :NPAN] = own_ref[...]
+            obuf[slot, WIDTH:, :NPAN] = b_ref[WIDTH:, :NPAN] - top[WIDTH:]
+
         store(i).start()
         return carry
 
     lax.fori_loop(0, nsteps, step, 0)
-    for i in range(nsteps):
+    for i in range(nsteps - nslots, nsteps):
         store(i).wait()
 
 
@@ -481,31 +495,33 @@
         buf = lambda *shape: pltpu.VMEM(shape, jnp.float32)
         dma = lambda *shape: pltpu.SemaphoreType.DMA(shape)
         bf16 = pltpu.VMEM((nloc, nrow), jnp.bfloat16)
-        p_t, xt, fix, own, tfac, tau = pl.pallas_call(
+        kept = lambda *shape: pltpu.VMEM(shape, jnp.float32)
+        b_kept, p_kept, xt, fix, own, tfac, tau = pl.pallas_call(
             panel_kernel,
             in_specs=[hbm],
-            out_specs=(hbm, vmem, vmem, vmem, vmem, vmem),
-            out_shape=(full((NPAN, nrow)), full((nloc, NPAN)), full((NPAN, NPAN)), full((WIDTH, NPAN)), full((PANELS, WIDTH, WIDTH)), full((1, NPAN))),
+            out_specs=(vmem, vmem, vmem, vmem, vmem, vmem, vmem),
+            out_shape=(kept(nloc, nrow), kept(NPAN, nrow), kept(nloc, NPAN), kept(NPAN, NPAN), kept(WIDTH, NPAN), kept(PANELS, WIDTH, WIDTH), kept(1, NPAN)),
             scratch_shapes=[
-                buf(nloc, nrow), bf16, bf16, bf16, buf(NPAN, nrow), buf(NPAN, nloc), buf(3, NPAN, nloc),
+                bf16, bf16, bf16, buf(NPAN, nloc), buf(3, NPAN, nloc),
                 buf(ROWS, NPAN, NPAN), buf(2, NPAN, NPAN), buf(NPAN, NPAN), buf(nloc, NPAN),
                 buf(NPAN, NPAN), buf(NPAN, NPAN), buf(NPAN, NPAN),
-                pltpu.SemaphoreType.DMA, dma(12), pltpu.SemaphoreType.DMA,
+                pltpu.SemaphoreType.DMA, dma(12),
                 dma(COLS, QUARTERS), dma(2, COLS, QUARTERS), dma(COLS), dma(COLS - 1), pltpu.SemaphoreType.DMA, dma(ROWS - 1), pltpu.SemaphoreType.DMA, dma(ROWS - 1),
-                dma(ROWS), dma(ROWS - 1), dma(2), dma(COLS - 1), dma(3, 3), dma(3, 3),
+                dma(ROWS), dma(ROWS - 1), dma(2), dma(COLS - 1), dma(2), dma(2), dma(3, 3), dma(3, 3),
             ],
-            compiler_params=pltpu.CompilerParams(collective_id=0, has_side_effects=True, vmem_limit_bytes=60 * 1024 * 1024),
+            compiler_params=pltpu.CompilerParams(collective_id=0, has_side_effects=True, vmem_limit_bytes=44 * 1024 * 1024),
             name='panels',
         )(b_t)
-        steps = 8
+        slots, chunk = 3, 1024
         out, tfac, tau = pl.pallas_call(
             update_kernel,
-            in_specs=[hbm, hbm, vmem, vmem, vmem, vmem, vmem],
+            in_specs=[vmem] * 7,
             out_specs=(hbm, vmem, vmem),
             out_shape=(full((nloc, nrow)), full((PANELS, WIDTH, WIDTH)), full((1, NPAN))),
-            scratch_shapes=[buf(nloc, nrow), buf(NPAN, nrow), pltpu.VMEM((nloc, 6 * NPAN), jnp.bfloat16), dma(steps), dma(steps), dma(steps)],
+            scratch_shapes=[buf(slots, nloc, chunk), pltpu.VMEM((nloc, 6 * NPAN), jnp.bfloat16), dma(slots)],
+            compiler_params=pltpu.CompilerParams(vmem_limit_bytes=20 * 1024 * 1024),
             name='update',
-        )(b_t, p_t, xt, fix, own, tfac, tau)
+        )(b_kept, p_kept, xt, fix, own, tfac, tau)
         return out.reshape(nblk, width, nrow).transpose(2, 0, 1), tau.reshape(NPAN), tfac
 
     return jax.shard_map(device_fn, mesh=mesh, in_specs=(block_spec,), out_specs=(block_spec, P('batch'), P('batch', None, None)), check_vma=False)

time: 86.1 us -> 81.4 us (0.945)
  Pallas kernels: 85.2 us -> 80.4 us
    pallas_call x2, Pallas kernels: 85.2 us -> 80.4 us  [the longest x1 71.4 us: device_fn(): pl.pallas_call(panel_kernel, in_specs=[hbm], out_specs=(vmem, vmem, vmem,...]
where the time goes in v4:
time: 81.4 us; the launch traced here: 81.2 us
  Pallas kernels  80.4 us (99%)
    pallas_call x1, Pallas kernels, device_fn(): pl.pallas_call(panel_kernel, in_specs=[hbm], out_specs=(vmem, vmem, vmem,...  71.4 us
    pallas_call x1, Pallas kernels, device_fn(): pl.pallas_call(update_kernel, in_specs=[vmem] * 7, out_specs=(hbm, vmem,...  9.01 us

profile of v4, /device:TPU:1, one launch (start us, length us, event | category | flops | bytes accessed | tf_op | source)
XLA Modules:
  0.0 81.2 jit_solution(17282975397877583649)
XLA Ops:
  0.6 71.4 %panels.1 = (f32[512,6144]{1,0:T(8,128)S(1)}, f32[128,6144]{1,0:T(8,128)S(1)}, f32[512,128]{1,0:T(8,128)S(1)}, f32[128,128]{1,0:T(8,128)S(1)}, f32[32,128]{1,0:T...) custom-call(f32[512,6144]{1,0:T(8,128)} %bitcast.7), custom_call_target="tpu_custom_call" | custom-call | tf_op jit(solution)/shard_map/panels/pallas_call | solution.py:499
  72.1 9.0 %update.1 = (f32[512,6144]{1,0:T(8,128)}, f32[4,32,32]{2,1,0:T(8,128)}, f32[1,128]{1,0:T(1,128)}) custom-call(f32[512,6144]{1,0:T(8,128)S(1)} %get-tuple-element.13.b_ref, f32[128,6144]{1,0:T(8,128)S(1)} %get-tuple-element.14.p_ref, f32[512,128]{1,0:T(8,128)S(1)} %get-tuple-element.15.xt_ref, f32[128,128]{1,0:T(8,128)S(1)} %get-tuple-element.16.fix_ref, ...), custom_call_target="tpu_custom_call" | custom-call | tf_op jit(solution)/shard_map/update/pallas_call | solution.py:516

commit v5 on v4

--- a/solution.py
+++ b/solution.py
@@ -67,14 +67,26 @@
 def upper_inverse(mat):
     rows = lax.broadcasted_iota(jnp.int32, mat.shape, 0)
     cols = lax.broadcasted_iota(jnp.int32, mat.shape, 1)
-    inv = jnp.where(rows == cols, 1.0 / jnp.where(rows == cols, mat, 1.0), 0.0)
-    size = 1
+    eye = jnp.where(rows == cols, 1.0, 0.0)
+    diag = jnp.where(rows == cols, mat, 0.0)
+    down = 1.0 / jnp.sum(diag, axis=1, keepdims=True)
+    across = 1.0 / jnp.sum(diag, axis=0, keepdims=True)
+    power = jnp.where((cols > rows) & (rows // WIDTH == cols // WIDTH), mat, 0.0) * -down
+    inv = eye + power
+    size = 2
+    while size < WIDTH:
+        power = dot(power, power)
+        inv = dot(inv, eye + power)
+        size *= 2
+    inv = inv * across
+    size = WIDTH
     while size < mat.shape[0]:
         pair = (rows // (2 * size) == cols // (2 * size)) & ((rows // size) % 2 == 0) & ((cols // size) % 2 == 1)
         off = jnp.where(pair, mat, 0.0)
         inv = inv - dot(dot(inv, off), inv)
         size *= 2
     return inv
+
 
 COLS = 4
 ROWS = 4
@@ -437,16 +449,12 @@
 
 
 def update_kernel(b_ref, p_ref, xt_ref, fix_ref, own_ref, tfac_ref, tau_in, out_hbm, t_ref, tau_ref, obuf, xcat, out_sem):
-    nslots, _, chunk = obuf.shape
+    chunk = obuf.shape[2]
     nsteps = b_ref.shape[1] // chunk
     first = lax.axis_index('row') == 0
 
-    def lanes_of(i):
-        return pl.ds(pl.multiple_of(i * chunk, chunk), chunk)
-
     def store(i):
-        slot = lax.rem(i, nslots)
-        return pltpu.make_async_copy(obuf.at[slot], out_hbm.at[:, lanes_of(i)], out_sem.at[slot])
+        return pltpu.make_async_copy(obuf.at[i], out_hbm.at[:, pl.ds(i * chunk, chunk)], out_sem.at[i])
 
     t_ref[...] = tfac_ref[...]
     tau_ref[...] = tau_in[...]
@@ -454,31 +462,22 @@
     for slot, part in enumerate((hi, hi, hi, mid, mid, lo)):
         xcat[:, slot * NPAN:(slot + 1) * NPAN] = part
 
-    def step(i, carry):
-        lanes = lanes_of(i)
+    for i in range(nsteps):
+        lanes = slice(i * chunk, (i + 1) * chunk)
         hi, mid, lo = split3(p_ref[:, lanes])
         pcat = jnp.concatenate([hi, mid, lo, hi, mid, hi], axis=0)
-
-        @pl.when(i >= nslots)
-        def _():
-            store(i - nslots).wait()
-
-        slot = lax.rem(i, nslots)
         prod = lax.dot_general(xcat[...], pcat, NN, preferred_element_type=jnp.float32)
-        obuf[slot, :WIDTH, :] = -prod[:WIDTH]
-        obuf[slot, WIDTH:, :] = b_ref[WIDTH:, lanes] - prod[WIDTH:]
-
-        @pl.when(first & (i == 0))
-        def _():
-            top = dot(xt_ref[...], fix_ref[...])
-            obuf[slot, :WIDTH, :NPAN] = own_ref[...]
-            obuf[slot, WIDTH:, :NPAN] = b_ref[WIDTH:, :NPAN] - top[WIDTH:]
-
+        obuf[i, :WIDTH, :] = -prod[:WIDTH]
+        obuf[i, WIDTH:, :] = b_ref[WIDTH:, lanes] - prod[WIDTH:]
+        if i == 0:
+            @pl.when(first)
+            def _():
+                top = dot(xt_ref[...], fix_ref[...])
+                obuf[0, :WIDTH, :NPAN] = own_ref[...]
+                obuf[0, WIDTH:, :NPAN] = b_ref[WIDTH:, :NPAN] - top[WIDTH:]
         store(i).start()
-        return carry
-
-    lax.fori_loop(0, nsteps, step, 0)
-    for i in range(nsteps - nslots, nsteps):
+
+    for i in range(nsteps):
         store(i).wait()
 
 
@@ -512,14 +511,15 @@
             compiler_params=pltpu.CompilerParams(collective_id=0, has_side_effects=True, vmem_limit_bytes=44 * 1024 * 1024),
             name='panels',
         )(b_t)
-        slots, chunk = 3, 1024
+        chunk = 512
+        slots = nrow // chunk
         out, tfac, tau = pl.pallas_call(
             update_kernel,
             in_specs=[vmem] * 7,
             out_specs=(hbm, vmem, vmem),
             out_shape=(full((nloc, nrow)), full((PANELS, WIDTH, WIDTH)), full((1, NPAN))),
             scratch_shapes=[buf(slots, nloc, chunk), pltpu.VMEM((nloc, 6 * NPAN), jnp.bfloat16), dma(slots)],
-            compiler_params=pltpu.CompilerParams(vmem_limit_bytes=20 * 1024 * 1024),
+            compiler_params=pltpu.CompilerParams(vmem_limit_bytes=24 * 1024 * 1024),
             name='update',
         )(b_kept, p_kept, xt, fix, own, tfac, tau)
         return out.reshape(nblk, width, nrow).transpose(2, 0, 1), tau.reshape(NPAN), tfac

time: 81.4 us -> 78.7 us (0.967)
  Pallas kernels: 80.4 us -> 77.7 us
    pallas_call x1, Pallas kernels: 9.01 us -> 7.2 us  [device_fn(): pl.pallas_call(update_kernel, in_specs=[vmem] * 7, out_specs=(hbm, vmem,...]
    pallas_call x1, Pallas kernels: 71.4 us -> 70.5 us  [device_fn(): pl.pallas_call(panel_kernel, in_specs=[hbm], out_specs=(vmem, vmem, vmem,...]
where the time goes in v5:
time: 78.7 us; the launch traced here: 78.5 us
  Pallas kernels  77.7 us (99%)
  between operations  0.82 us (1%)
    pallas_call x1, Pallas kernels, device_fn(): pl.pallas_call(panel_kernel, in_specs=[hbm], out_specs=(vmem, vmem, vmem,...  70.5 us
    pallas_call x1, Pallas kernels, device_fn(): pl.pallas_call(update_kernel, in_specs=[vmem] * 7, out_specs=(hbm, vmem,...  7.2 us

profile of v5, /device:TPU:1, one launch (start us, length us, event | category | flops | bytes accessed | tf_op | source)
XLA Modules:
  0.0 78.5 jit_solution(15302011922035439651)
XLA Ops:
  0.6 70.5 %panels.1 = (f32[512,6144]{1,0:T(8,128)S(1)}, f32[128,6144]{1,0:T(8,128)S(1)}, f32[512,128]{1,0:T(8,128)S(1)}, f32[128,128]{1,0:T(8,128)S(1)}, f32[32,128]{1,0:T...) custom-call(f32[512,6144]{1,0:T(8,128)} %bitcast.7), custom_call_target="tpu_custom_call" | custom-call | tf_op jit(solution)/shard_map/panels/pallas_call | solution.py:498
  71.2 7.2 %update.1 = (f32[512,6144]{1,0:T(8,128)}, f32[4,32,32]{2,1,0:T(8,128)}, f32[1,128]{1,0:T(1,128)}) custom-call(f32[512,6144]{1,0:T(8,128)S(1)} %get-tuple-element.13.b_ref, f32[128,6144]{1,0:T(8,128)S(1)} %get-tuple-element.14.p_ref, f32[512,128]{1,0:T(8,128)S(1)} %get-tuple-element.15.xt_ref, f32[128,128]{1,0:T(8,128)S(1)} %get-tuple-element.16.fix_ref, ...), custom_call_target="tpu_custom_call" | custom-call | tf_op jit(solution)/shard_map/update/pallas_call | solution.py:516

commit v6 on v5

--- a/solution.py
+++ b/solution.py
@@ -414,7 +414,7 @@
         for dr in range(1, ROWS):
             h_copy(piece, dr).wait()
     total = (hacc[...] - corr) + (hslot[0] + hslot[1] + hslot[2])
-    xt_ref[...] = lax.dot_general(total, gram[...], (((0,), (1,)), ((), ())), precision=HIGHEST, preferred_element_type=jnp.float32)
+    xt_ref[...] = dot(gram[...], total).T
     xt_ref[:WIDTH, :] = -work[pl.ds(own_base, WIDTH), :]
 
     def sent(panel, parts, direction):

time: 78.7 us -> 78.5 us (level)
  no operation moved by 1% of the time
where the time goes in v6:
time: 78.5 us; the launch traced here: 78.3 us
  Pallas kernels  77.5 us (99%)
  between operations  0.82 us (1%)
    pallas_call x1, Pallas kernels, device_fn(): pl.pallas_call(panel_kernel, in_specs=[hbm], out_specs=(vmem, vmem, vmem,...  70.3 us
    pallas_call x1, Pallas kernels, device_fn(): pl.pallas_call(update_kernel, in_specs=[vmem] * 7, out_specs=(hbm, vmem,...  7.2 us

profile of v6, /device:TPU:1, one launch (start us, length us, event | category | flops | bytes accessed | tf_op | source)
XLA Modules:
  0.0 78.3 jit_solution(11505617781050175926)
XLA Ops:
  0.6 70.3 %panels.1 = (f32[512,6144]{1,0:T(8,128)S(1)}, f32[128,6144]{1,0:T(8,128)S(1)}, f32[512,128]{1,0:T(8,128)S(1)}, f32[128,128]{1,0:T(8,128)S(1)}, f32[32,128]{1,0:T...) custom-call(f32[512,6144]{1,0:T(8,128)} %bitcast.7), custom_call_target="tpu_custom_call" | custom-call | tf_op jit(solution)/shard_map/panels/pallas_call | solution.py:498
  70.9 7.2 %update.1 = (f32[512,6144]{1,0:T(8,128)}, f32[4,32,32]{2,1,0:T(8,128)}, f32[1,128]{1,0:T(1,128)}) custom-call(f32[512,6144]{1,0:T(8,128)S(1)} %get-tuple-element.13.b_ref, f32[128,6144]{1,0:T(8,128)S(1)} %get-tuple-element.14.p_ref, f32[512,128]{1,0:T(8,128)S(1)} %get-tuple-element.15.xt_ref, f32[128,128]{1,0:T(8,128)S(1)} %get-tuple-element.16.fix_ref, ...), custom_call_target="tpu_custom_call" | custom-call | tf_op jit(solution)/shard_map/update/pallas_call | solution.py:516
